TPU v7x, 128 devices: a whole 4x4x4 slice. The times are simulated.
128 devices in a mesh: seqs: 1, rows: 2 (over core), states: 64 (over z, y, x).
Axes of the slice: x: 4, y: 4, z: 4, core: 2. Of those that a mesh axis runs over, the one named last changes fastest.
Arguments:
- trans_mat: bfloat16 [16384, 2, 8192], P('rows', None, 'states')
- emit_mat: bfloat16 [16384, 10000], P(('rows', 'states'))
- init_dist: float32 [16384], P(('rows', 'states'))
- tokens: int32 [16, 128], P('seqs')
- lengths: int32 [16], P('seqs')
Outputs:
- output 1: float32 [16], P('seqs')
- output 2: float32 [16, 16384], P('seqs', ('rows', 'states'))
All inputs are finite; a program needn't handle non-finite values.
Results may differ from a plain program's by a relative error of at most 0.001.
Values are sent between devices in bfloat16 or wider.
A program may use at most 1 GiB of HBM per device.

v0:
```python
import jax
import jax.numpy as jnp
from jax import lax
from jax.sharding import PartitionSpec as P


def solution(mesh):
    vec_axes = ('rows', 'states')

    def local_forward(trans_blk, emit_blk, init_blk, tokens, lengths):
        n_steps = tokens.shape[1]
        emis_all = jnp.transpose(jnp.take(emit_blk, tokens, axis=1), (2, 1, 0))
        first_raw = init_blk[None, :] * emis_all[0].astype(jnp.float32)
        norm_c = lax.psum(jnp.sum(first_raw, axis=1), vec_axes)
        alpha_init = first_raw / norm_c[:, None]
        loglik_init = jnp.log(norm_c)

        def one_step(state_in, inputs):
            alpha_cur, loglik = state_in
            emis_t, t_index = inputs
            gathered = lax.all_gather(alpha_cur.astype(jnp.bfloat16), 'states', axis=1, tiled=True)
            part_sum = jnp.einsum('bk,kaq->baq', gathered, trans_blk, preferred_element_type=jnp.float32)
            mix_sum = lax.psum_scatter(part_sum, 'rows', scatter_dimension=1, tiled=True)[:, 0, :]
            raw_next = mix_sum * emis_t.astype(jnp.float32)
            norm_step = lax.psum(jnp.sum(raw_next, axis=1), vec_axes)
            active = t_index < lengths
            alpha_cur = jnp.where(active[:, None], raw_next / norm_step[:, None], alpha_cur)
            loglik = loglik + jnp.where(active, jnp.log(norm_step), 0.0)
            return (alpha_cur, loglik), None

        scan_out = lax.scan(one_step, (alpha_init, loglik_init), (emis_all[1:], jnp.arange(1, n_steps)))
        alpha_last, loglik = scan_out[0]
        return loglik, alpha_last

    return jax.shard_map(local_forward, mesh=mesh, in_specs=(P('rows', None, 'states'), P(vec_axes, None), P(vec_axes), P('seqs', None), P('seqs')), out_specs=(P('seqs'), P('seqs', vec_axes)), check_vma=False)
```

profile of v0, /device:TPU:1, one launch (start us, length us, event | category | flops | bytes accessed | tf_op | source)
XLA Modules:
  0.0 31843.4 jit_solution(12857651896352183495)
XLA Ops:
  92.9 31743.1 %while.12 = (s32[]{:T(128)}, f32[16,128]{1,0:T(8,128)S(1)}, f32[16]{0:T(128)S(1)}, s32[127]{0:T(128)S(1)}, s32[16]{0:T(128)S(1)}, /*index=5*/bf16[8192,2,128]{2,...) while((s32[]{:T(128)}, f32[16,128]{1,0:T(8,128)S(1)}, f32[16]{0:T(128)S(1)}, s32[127]{0:T(128)S(1)}, ...), condition=%wide.region_6.7_spmd, body=%wide.region_2.6_spmd.sunk | while | flops 67125296 | bytes 4866749 | solution.py:31
  92.9 145.6 all_gather.4
  342.8 145.6 all_gather.4
  842.7 145.6 all_gather.4
  1342.6 145.6 all_gather.4
  1842.5 145.6 all_gather.4
  2342.4 145.6 all_gather.4
  2842.3 145.6 all_gather.4
  3342.2 145.6 all_gather.4
  3842.1 145.6 all_gather.4
  4342.0 145.6 all_gather.4
  4841.9 145.6 all_gather.4
  5341.8 145.6 all_gather.4
  5841.7 145.6 all_gather.4
  6341.6 145.6 all_gather.4
  6841.5 145.6 all_gather.4
  7341.4 145.6 all_gather.4
  7841.2 145.6 all_gather.4
  8341.1 145.6 all_gather.4
  8841.0 145.6 all_gather.4
  9340.9 145.6 all_gather.4
  9840.8 145.6 all_gather.4
  10340.7 145.6 all_gather.4
  10840.6 145.6 all_gather.4
  11340.5 145.6 all_gather.4
  11840.4 145.6 all_gather.4
  12340.3 145.6 all_gather.4
  12840.2 145.6 all_gather.4
  13340.1 145.6 all_gather.4
  13840.0 145.6 all_gather.4
  14339.8 145.6 all_gather.4
  14839.7 145.6 all_gather.4
  15339.6 145.6 all_gather.4
  15839.5 145.6 all_gather.4
  16339.4 145.6 all_gather.4
  16839.3 145.6 all_gather.4
  17339.2 145.6 all_gather.4
  17839.1 145.6 all_gather.4
  18339.0 145.6 all_gather.4
  18838.9 145.6 all_gather.4
  19338.7 145.6 all_gather.4
  19838.7 145.6 all_gather.4
  20338.5 145.6 all_gather.4
  20838.4 145.6 all_gather.4
  21338.3 145.6 all_gather.4
  21838.2 145.6 all_gather.4
  22338.1 145.6 all_gather.4
  22838.0 145.6 all_gather.4
  23337.9 145.6 all_gather.4
  23837.8 145.6 all_gather.4
  24337.7 145.6 all_gather.4
  24837.6 145.6 all_gather.4
  25337.4 145.6 all_gather.4
  25837.3 145.6 all_gather.4
  26337.2 145.6 all_gather.4
  26837.1 145.6 all_gather.4
  27337.0 145.6 all_gather.4
  27836.9 145.6 all_gather.4
  28336.8 145.6 all_gather.4
  28836.7 145.6 all_gather.4
  29336.6 145.6 all_gather.4
  29836.5 145.6 all_gather.4
  30336.4 145.6 all_gather.4
  31336.1 145.6 all_gather.4
  (1358 shorter events, 22652.1 us)
Async XLA Ops:
  342.7 181.2 reduce-scatter.2.cloned.1.call-start
  592.7 181.2 reduce-scatter.2.cloned.1.call-start
  842.6 181.2 reduce-scatter.2.cloned.1.call-start
  1092.6 181.2 reduce-scatter.2.cloned.1.call-start
  1342.5 181.2 reduce-scatter.2.cloned.1.call-start
  1592.5 181.2 reduce-scatter.2.cloned.1.call-start
  1842.4 181.2 reduce-scatter.2.cloned.1.call-start
  2342.3 181.2 reduce-scatter.2.cloned.1.call-start
  2842.3 181.2 reduce-scatter.2.cloned.1.call-start
  3092.2 181.2 reduce-scatter.2.cloned.1.call-start
  3342.2 181.2 reduce-scatter.2.cloned.1.call-start
  3592.1 181.2 reduce-scatter.2.cloned.1.call-start
  3842.1 181.2 reduce-scatter.2.cloned.1.call-start
  4092.0 181.2 reduce-scatter.2.cloned.1.call-start
  4342.0 181.2 reduce-scatter.2.cloned.1.call-start
  4591.9 181.2 reduce-scatter.2.cloned.1.call-start
  4841.8 181.2 reduce-scatter.2.cloned.1.call-start
  5341.7 181.2 reduce-scatter.2.cloned.1.call-start
  5591.7 181.2 reduce-scatter.2.cloned.1.call-start
  5841.6 181.2 reduce-scatter.2.cloned.1.call-start
  6341.5 181.2 reduce-scatter.2.cloned.1.call-start
  6591.5 181.2 reduce-scatter.2.cloned.1.call-start
  6841.4 181.2 reduce-scatter.2.cloned.1.call-start
  7341.3 181.2 reduce-scatter.2.cloned.1.call-start
  7591.2 181.2 reduce-scatter.2.cloned.1.call-start
  7841.2 181.2 reduce-scatter.2.cloned.1.call-start
  8091.1 181.2 reduce-scatter.2.cloned.1.call-start
  8341.1 181.2 reduce-scatter.2.cloned.1.call-start
  9340.8 181.2 reduce-scatter.2.cloned.1.call-start
  9590.8 181.2 reduce-scatter.2.cloned.1.call-start
  9840.7 181.2 reduce-scatter.2.cloned.1.call-start
  10340.7 181.2 reduce-scatter.2.cloned.1.call-start
  10840.5 181.2 reduce-scatter.2.cloned.1.call-start
  11840.3 181.2 reduce-scatter.2.cloned.1.call-start
  12340.2 181.2 reduce-scatter.2.cloned.1.call-start
  12590.2 181.2 reduce-scatter.2.cloned.1.call-start
  12840.1 181.2 reduce-scatter.2.cloned.1.call-start
  13839.9 181.2 reduce-scatter.2.cloned.1.call-start
  14339.8 181.2 reduce-scatter.2.cloned.1.call-start
  15839.4 181.2 reduce-scatter.2.cloned.1.call-start
  16339.3 181.2 reduce-scatter.2.cloned.1.call-start
  17089.2 181.2 reduce-scatter.2.cloned.1.call-start
  17839.0 181.2 reduce-scatter.2.cloned.1.call-start
  18338.9 181.2 reduce-scatter.2.cloned.1.call-start
  18838.8 181.2 reduce-scatter.2.cloned.1.call-start
  19338.7 181.2 reduce-scatter.2.cloned.1.call-start
  20338.5 181.2 reduce-scatter.2.cloned.1.call-start
  20838.4 181.2 reduce-scatter.2.cloned.1.call-start
  21338.3 181.2 reduce-scatter.2.cloned.1.call-start
  21838.2 181.2 reduce-scatter.2.cloned.1.call-start
  22338.1 181.2 reduce-scatter.2.cloned.1.call-start
  22838.0 181.2 reduce-scatter.2.cloned.1.call-start
  23837.7 181.2 reduce-scatter.2.cloned.1.call-start
  24337.6 181.2 reduce-scatter.2.cloned.1.call-start
  24837.5 181.2 reduce-scatter.2.cloned.1.call-start
  25337.4 181.2 reduce-scatter.2.cloned.1.call-start
  25837.3 181.2 reduce-scatter.2.cloned.1.call-start
  27336.9 181.2 reduce-scatter.2.cloned.1.call-start
  27836.8 181.2 reduce-scatter.2.cloned.1.call-start
  28836.6 181.2 reduce-scatter.2.cloned.1.call-start
  29836.4 181.2 reduce-scatter.2.cloned.1.call-start
  30336.3 181.2 reduce-scatter.2.cloned.1.call-start
  30836.2 181.2 reduce-scatter.2.cloned.1.call-start
  31336.1 181.2 reduce-scatter.2.cloned.1.call-start
  (69 other events, 11441.4 us)
Sparse Core Ops, SparseCore 0:
  741.9 31.8 reduce-scatter.1
  991.9 31.8 reduce-scatter.1
  1741.7 31.8 reduce-scatter.1
  1991.7 31.8 reduce-scatter.1
  2241.6 31.8 reduce-scatter.1
  2491.6 31.8 reduce-scatter.1
  2741.6 31.8 reduce-scatter.1
  2991.6 31.8 reduce-scatter.1
  3741.4 31.8 reduce-scatter.1
  3991.3 31.8 reduce-scatter.1
  4241.3 31.8 reduce-scatter.1
  4491.2 31.8 reduce-scatter.1
  4741.2 31.8 reduce-scatter.1
  4991.1 31.8 reduce-scatter.1
  5241.0 31.8 reduce-scatter.1
  5491.0 31.8 reduce-scatter.1
  6240.8 31.8 reduce-scatter.1
  6490.8 31.8 reduce-scatter.1
  6740.7 31.8 reduce-scatter.1
  6990.7 31.8 reduce-scatter.1
  7240.6 31.8 reduce-scatter.1
  7740.5 31.8 reduce-scatter.1
  7990.5 31.8 reduce-scatter.1
  8740.3 31.8 reduce-scatter.1
  8990.2 31.8 reduce-scatter.1
  9490.1 31.8 reduce-scatter.1
  9740.1 31.8 reduce-scatter.1
  9990.0 31.8 reduce-scatter.1
  10240.0 31.8 reduce-scatter.1
  10489.9 31.8 reduce-scatter.1
  10739.9 31.8 reduce-scatter.1
  11239.7 31.8 reduce-scatter.1
  11489.7 31.8 reduce-scatter.1
  11989.6 31.8 reduce-scatter.1
  12489.5 31.8 reduce-scatter.1
  12739.4 31.8 reduce-scatter.1
  12989.4 31.8 reduce-scatter.1
  13489.3 31.8 reduce-scatter.1
  13739.2 31.8 reduce-scatter.1
  13989.2 31.8 reduce-scatter.1
  14239.1 31.8 reduce-scatter.1
  14489.0 31.8 reduce-scatter.1
  14739.0 31.8 reduce-scatter.1
  15238.9 31.8 reduce-scatter.1
  15488.8 31.8 reduce-scatter.1
  15738.8 31.8 reduce-scatter.1
  16238.7 31.8 reduce-scatter.1
  16488.6 31.8 reduce-scatter.1
  16738.5 31.8 reduce-scatter.1
  16988.5 31.8 reduce-scatter.1
  17238.4 31.8 reduce-scatter.1
  17488.4 31.8 reduce-scatter.1
  17738.4 31.8 reduce-scatter.1
  17988.3 31.8 reduce-scatter.1
  18238.2 31.8 reduce-scatter.1
  18738.1 31.8 reduce-scatter.1
  18988.1 31.8 reduce-scatter.1
  19238.0 31.8 reduce-scatter.1
  19737.9 31.8 reduce-scatter.1
  19987.9 31.8 reduce-scatter.1
  20237.8 31.8 reduce-scatter.1
  20487.8 31.8 reduce-scatter.1
  20737.7 31.8 reduce-scatter.1
  20987.6 31.8 reduce-scatter.1
  (63 shorter events, 2003.2 us)
where the time goes:
time: 31900 us; the launch traced here: 31800 us
  blocking collectives  27000 us (85%)
  waiting for transfers between devices  3990 us (13%)
  matrix products  438 us (1%)
    all_gather x127, blocking collectives, one_step(): lax.all_gather(alpha_cur.astype(jnp.bfloat16), 'states', axis=1, tiled=True)  18500 us
    psum x127, blocking collectives, one_step(): norm_step = lax.psum(jnp.sum(raw_next, axis=1), vec_axes)  8450 us
    reduce_scatter x127, waiting for transfers between devices, one_step(): lax.psum_scatter(part_sum, 'rows', scatter_dimension=1, tiled=True)[:, 0, :]  3990 us
  transfers between devices with their start and end apart: 127, of which 127 were waited for; matrix products, arithmetic and copies ran while one was open for 0% of the time, Pallas kernels for 0%

commit v1 on v0

v1 whole, which is shorter than its diff:
```python
import functools

import jax
import jax.numpy as jnp
from jax import lax
from jax.experimental import pallas as pl
from jax.experimental.pallas import tpu as pltpu
from jax.sharding import PartitionSpec as P

CHIPS = (4, 4, 4)
SB = 128
F32 = jnp.float32
BF16 = jnp.bfloat16


def ring_distance(offset, n):
    return min(offset, n - offset)


def forward_kernel(dims, n_steps, a_ref, e_ref, r0_ref, lencol_ref, lenrow_ref, alpha_ref, ll_ref,
                   a_loc, e_loc, r_in, c_in, p_in, u_in, u_out, a_bf, alpha_acc, ll_acc, fin_alpha, fin_ll,
                   a_sem, a_send, e_sem, e_send, r0_sem, r0_send, own_sem,
                   g_recv, g_send, c_recv, c_send, u_recv, u_send, p_recv, p_send, f_recv, f_send):
    nz, ny, nx = dims
    plane = ny * nx
    batch = r0_ref.shape[0]
    half = plane * SB
    core = lax.axis_index('rows')
    me = lax.axis_index('states')
    z = me // plane
    yx = me % plane
    y = yx // nx
    x = yx % nx
    far_z = sorted(range(1, nz), key=lambda d: -ring_distance(d, nz))
    far_yx = sorted(((j, i) for j in range(ny) for i in range(nx) if j or i),
                    key=lambda o: -(ring_distance(o[0], ny) + ring_distance(o[1], nx)))

    def line_peer(dz):
        return ((z + dz) % nz) * plane + yx

    def plane_peer(dy, dx):
        return z * plane + ((y + dy) % ny) * nx + (x + dx) % nx

    def remote(src, dst, send, recv, state):
        return pltpu.make_async_remote_copy(src_ref=src, dst_ref=dst, send_sem=send, recv_sem=recv,
                                            device_id={'rows': 1, 'states': state},
                                            device_id_type=pl.DeviceIdType.MESH)

    def wait_bytes(ref, sem):
        pltpu.make_async_copy(ref, ref, sem).wait()

    def hand_over(h):
        copies = []
        for k in range(nz):
            if h == 1 and k == 0:
                continue
            dz = (nz - k) % nz
            rows = pl.ds(((z + k) % nz) * half, half)
            copies.append(remote(a_ref.at[rows], a_loc.at[dz, pl.ds(h * half, half)],
                                 a_send.at[k], a_sem.at[dz, h], line_peer(k)))
        for k in range(nz):
            if h == 1 and k == 0:
                continue
            dz = (nz - k) % nz
            copies.append(remote(e_ref, e_loc.at[dz, h], e_send.at[k], e_sem.at[dz, h], line_peer(k)))
        return copies

    @pl.when(core == 0)
    def helper():
        first = remote(r0_ref, r_in.at[0, yx, 0], r0_send, r0_sem, me)
        first.start()
        copies = hand_over(0)
        for copy in copies:
            copy.start()
        first.wait_send()
        for copy in copies:
            copy.wait_send()
        wait_bytes(fin_alpha, f_recv.at[0])
        wait_bytes(fin_ll, f_recv.at[1])
        alpha_ref[...] = fin_alpha[...]
        ll_ref[...] = fin_ll[...]

    @pl.when(core == 1)
    def owner():
        eye = (lax.broadcasted_iota(jnp.int32, (batch, SB), 0)
               == lax.broadcasted_iota(jnp.int32, (batch, SB), 1))

        def as_row(tile):
            col = jnp.sum(tile, axis=1, keepdims=True)
            return jnp.sum(jnp.where(eye, col, 0.0), axis=0, keepdims=True)

        def as_col(row):
            return jnp.sum(jnp.where(eye, row, 0.0), axis=1, keepdims=True)

        def start_gather(slot):
            for dy, dx in far_yx:
                remote(r_in.at[slot, yx], r_in.at[slot, yx], g_send, g_recv.at[slot], plane_peer(dy, dx)).start()

        def start_norms(slot):
            for dy, dx in far_yx:
                remote(c_in.at[slot, yx], c_in.at[slot, yx], c_send, c_recv.at[slot], plane_peer(dy, dx)).start()

        def start_line_sums(slot):
            for dz in far_z:
                remote(p_in.at[slot, z], p_in.at[slot, z], p_send, p_recv.at[slot], line_peer(dz)).start()

        def finish_norm(slot):
            wait_bytes(p_in.at[slot, pl.ds(0, nz - 1)], p_recv.at[slot])
            c_in[slot, yx] = jnp.sum(p_in[slot], axis=0)
            start_norms(slot)

        others = pl.ds(0, plane - 1)

        def norm(slot):
            wait_bytes(c_in.at[slot, others], c_recv.at[slot])
            c_row = jnp.sum(c_in[slot], axis=0)
            return c_row, 1.0 / as_col(c_row)

        def keep(t, slot, c_row, inv):
            active = t < lencol_ref[...]
            for h in range(2):
                alpha_acc[h] = jnp.where(active, r_in[slot, yx, h] * inv, alpha_acc[h])
            ll_acc[...] = ll_acc[...] + jnp.where(t < lenrow_ref[...], jnp.log(c_row), 0.0)

        copies = hand_over(1)
        for copy in copies:
            copy.start()
        own = [pltpu.make_async_copy(a_ref.at[pl.ds(z * half, half)], a_loc.at[0, pl.ds(half, half)], own_sem.at[0]),
               pltpu.make_async_copy(e_ref, e_loc.at[0, 1], own_sem.at[1])]
        for copy in own:
            copy.start()
        alpha_acc[...] = jnp.zeros_like(alpha_acc)
        ll_acc[...] = jnp.zeros_like(ll_acc)
        r_in[0, yx, 1] = r0_ref[...]
        wait_bytes(r0_ref, r0_sem)
        p_in[0, z] = as_row(r_in[0, yx, 0] + r_in[0, yx, 1])
        start_line_sums(0)
        start_gather(0)
        finish_norm(0)
        wait_bytes(p_in.at[0, pl.ds(0, nz - 1)], p_send)
        for copy in own:
            copy.wait()
        for h in range(2):
            for dz in range(nz):
                if h == 1 and dz == 0:
                    continue
                wait_bytes(e_loc.at[dz, h], e_sem.at[dz, h])
                wait_bytes(a_loc.at[dz, pl.ds(h * half, half)], a_sem.at[dz, h])
        for copy in copies:
            copy.wait_send()

        def one_step(t, carry):
            cur = t % 2
            nxt = (t + 1) % 2
            c_row, inv = norm(cur)
            wait_bytes(r_in.at[cur, others], g_recv.at[cur])
            for src in range(plane):
                for h in range(2):
                    a_bf[:, pl.ds(h * half + src * SB, SB)] = (r_in[cur, src, h] * inv).astype(BF16)
            total = jnp.zeros((batch, SB), F32)
            for dz in far_z + [0]:
                part = jnp.dot(a_bf[...], a_loc[dz], preferred_element_type=F32)
                parts = (part[:, :SB], part[:, SB:])
                if dz:
                    for h in range(2):
                        u_out[dz - 1, h] = parts[h]
                    remote(u_out.at[dz - 1], u_in.at[nxt, nz - dz - 1], u_send, u_recv.at[nxt], line_peer(dz)).start()
                for h in range(2):
                    total = total + parts[h] * e_loc[dz, h, t + 1].astype(F32)
            p_in[nxt, z] = as_row(total)
            start_line_sums(nxt)
            wait_bytes(r_in.at[cur, others], g_send)
            wait_bytes(c_in.at[cur, others], c_send)
            keep(t, cur, c_row, inv)
            wait_bytes(u_in.at[nxt], u_recv.at[nxt])
            for h in range(2):
                u = parts[h]
                for k in range(nz - 1):
                    u = u + u_in[nxt, k, h]
                r_in[nxt, yx, h] = u * e_loc[0, h, t + 1].astype(F32)
            start_gather(nxt)
            finish_norm(nxt)
            wait_bytes(u_out, u_send)
            wait_bytes(p_in.at[nxt, pl.ds(0, nz - 1)], p_send)
            return carry

        lax.fori_loop(0, n_steps - 1, one_step, 0)
        last = (n_steps - 1) % 2
        c_row, inv = norm(last)
        wait_bytes(r_in.at[last, others], g_recv.at[last])
        keep(n_steps - 1, last, c_row, inv)
        wait_bytes(r_in.at[last, others], g_send)
        wait_bytes(c_in.at[last, others], c_send)

        def to_helper(src, dst, i):
            return pltpu.make_async_remote_copy(src_ref=src, dst_ref=dst, send_sem=f_send.at[i], recv_sem=f_recv.at[i],
                                                device_id={'rows': 0, 'states': me},
                                                device_id_type=pl.DeviceIdType.MESH)

        result = [to_helper(alpha_acc.at[0], fin_alpha, 0), to_helper(ll_acc, fin_ll, 1)]
        for copy in result:
            copy.start()
        alpha_ref[...] = alpha_acc[1]
        ll_ref[...] = ll_acc[...]
        for copy in result:
            copy.wait_send()


def solution(mesh):
    vec_axes = ('rows', 'states')
    nz, ny, nx = CHIPS
    plane = ny * nx

    def local_forward(trans_blk, emit_blk, init_blk, tokens, lengths):
        batch, n_steps = tokens.shape
        cols = 2 * SB
        a_blk = trans_blk.reshape(trans_blk.shape[0], cols)
        emis = jnp.transpose(jnp.take(emit_blk, tokens, axis=1), (2, 1, 0))
        first_raw = init_blk[None, :] * emis[0].astype(F32)
        len_col = jnp.broadcast_to(lengths[:, None], (batch, SB))
        len_row = jnp.pad(lengths, (0, SB - batch))[None, :]
        vmem = pl.BlockSpec(memory_space=pltpu.VMEM)
        hbm = pl.BlockSpec(memory_space=pl.ANY)
        dma = pltpu.SemaphoreType.DMA
        k_rows = 2 * plane * SB
        alpha, ll = pl.pallas_call(
            functools.partial(forward_kernel, CHIPS, n_steps),
            out_shape=(jax.ShapeDtypeStruct((batch, SB), F32), jax.ShapeDtypeStruct((1, SB), F32)),
            in_specs=[hbm, hbm, vmem, vmem, vmem],
            out_specs=(vmem, vmem),
            scratch_shapes=[
                pltpu.VMEM((nz, k_rows, cols), BF16),
                pltpu.VMEM((nz, 2, n_steps, batch, SB), BF16),
                pltpu.VMEM((2, plane, 2, batch, SB), F32),
                pltpu.VMEM((2, plane, 1, SB), F32),
                pltpu.VMEM((2, nz, 1, SB), F32),
                pltpu.VMEM((2, nz - 1, 2, batch, SB), F32),
                pltpu.VMEM((nz - 1, 2, batch, SB), F32),
                pltpu.VMEM((batch, k_rows), BF16),
                pltpu.VMEM((2, batch, SB), F32),
                pltpu.VMEM((1, SB), F32),
                pltpu.VMEM((batch, SB), F32),
                pltpu.VMEM((1, SB), F32),
                dma((nz, 2)), dma((nz,)), dma((nz, 2)), dma((nz,)), dma, dma, dma((2,)),
                dma((2,)), dma, dma((2,)), dma, dma((2,)), dma, dma((2,)), dma, dma((2,)), dma((2,)),
            ],
            compiler_params=pltpu.CompilerParams(has_side_effects=True, vmem_limit_bytes=48 * 1024 * 1024),
            cost_estimate=pl.CostEstimate(flops=2 * batch * (n_steps - 1) * nz * k_rows * cols,
                                          bytes_accessed=nz * k_rows * cols * 2, transcendentals=0),
        )(a_blk, emis, first_raw, len_col, len_row)
        return ll[0, :batch], alpha

    return jax.shard_map(local_forward, mesh=mesh, in_specs=(P('rows', None, 'states'), P(vec_axes, None), P(vec_axes), P('seqs', None), P('seqs')), out_specs=(P('seqs'), P('seqs', vec_axes)), check_vma=False)
```

time: 31900 us -> 1300 us (0.04)
  blocking collectives: 27000 us -> 0 us
  waiting for transfers between devices: 3990 us -> 0 us
  Pallas kernels: 0 us -> 1290 us
  matrix products: 438 us -> 0 us
    all_gather x127 -> x0, blocking collectives: 18500 us -> none  [one_step(): lax.all_gather(alpha_cur.astype(jnp.bfloat16), 'states', axis=1, tiled=True)]
    psum x128 -> x0, blocking collectives: 8520 us -> none  [the longest x127 8450 us: one_step(): norm_step = lax.psum(jnp.sum(raw_next, axis=1), vec_axes)]
    reduce_scatter x127 -> x0, waiting for transfers between devices: 3990 us -> none  [one_step(): lax.psum_scatter(part_sum, 'rows', scatter_dimension=1, tiled=True)[:, 0, :]]
    pallas_call x0 -> x1, Pallas kernels: none -> 1290 us  [local_forward(): pl.pallas_call(functools.partial(forward_kernel, CHIPS, n_steps), out_sha...]
    dot_general x127 -> x0, matrix products: 438 us -> none  [one_step(): jnp.einsum('bk,kaq->baq', gathered, trans_blk, preferred_element_type=jnp...]
  transfers between devices with their start and end apart: 127 -> 0, of which waited for: 127 -> 0; matrix products, arithmetic and copies ran while one was open for 0% -> 0% of each run, Pallas kernels for 0% -> 0%
where the time goes in v1:
time: 1300 us
  Pallas kernels  1290 us (99%)
    pallas_call x1, Pallas kernels, local_forward(): pl.pallas_call(functools.partial(forward_kernel, CHIPS, n_steps), out_sha...  1290 us

profile of v1, /device:TPU:1, one launch (start us, length us, event | category | flops | bytes accessed | tf_op | source)
XLA Modules:
  0.0 1302.5 jit_solution(5898979856241555437)
XLA Ops:
  0.6 0.0 copy-start
  0.6 0.0 copy-start.1
  0.7 0.8 pad_bitcast_fusion.lenrow_ref
  1.5 0.7 and_bitcast_fusion
  2.2 0.7 bitcast_clamp_fusion
  2.9 0.7 broadcast_in_dim.28.lencol_ref
  3.6 0.1 copy.8
  3.7 0.0 copy-done
  3.7 6.2 gather_fusion
  9.9 0.4 bitcast_select_fusion.e_ref
  10.3 0.0 copy-done.1
  10.3 2.7 copy.13
  13.1 1288.3 %shard_map.68 = (f32[16,128]{1,0:T(8,128)S(1)}, f32[1,128]{1,0:T(1,128)S(1)}) custom-call(bf16[8192,256]{1,0:T(8,128)(2,1)S(1)} %bitcast.20, bf16[128,16,128]{2,1,0:T(8,128)(2,1)S(1)} %bitcast_select_fusion.e_ref, f32[16,128]{1,0:T(8,128)S(1)} %convert_multiply_fusion.r0_ref, s32[16,128]{1,0:T(8,128)S(1)} %broadcast_in_dim.28.lencol_ref, ...), custom_call_target="tpu_custom_call" | custom-call | flops 17045651456 | bytes 8388608 | tf_op jit(solution)/shard_map/pallas_call | solution.py:226
  1301.4 0.5 slice_bitcast_fusion.1
  1301.9 0.6 copy.15
  (1 shorter events, 0.0 us)
Async XLA Ops:
  0.6 3.1 copy-start
  0.6 9.7 copy-start.1

commit v2 on v1

v2 whole, which is shorter than its diff:
```python
import functools

import jax
import jax.numpy as jnp
from jax import lax
from jax.experimental import pallas as pl
from jax.experimental.pallas import tpu as pltpu
from jax.sharding import PartitionSpec as P

CHIPS = (4, 4, 4)
SB = 128
LIFT = 2.0 ** 64
F32 = jnp.float32
BF16 = jnp.bfloat16


def ring_distance(offset, n):
    return min(offset, n - offset)


def forward_kernel(dims, n_steps, a_ref, e_ref, r0_ref, lencol_ref, lenrow_ref, alpha_ref, ll_ref,
                   a_loc, e_both, e_loc, w_loc, r_in, c_in, p_in, u_in, u_out, a_bf, alpha_acc, ll_acc, fin_alpha,
                   fin_ll, a_sem, a_send, e_pair, e_send, e_sem, r0_sem, r0_send, own_sem,
                   g_recv, g_send, c_recv, c_send, u_recv, u_send, p_recv, p_send, f_recv, f_send):
    nz, ny, nx = dims
    plane = nz * ny
    batch = r0_ref.shape[0]
    half = nx * SB
    block = plane
    rows = block * batch
    n_blocks = n_steps // block
    core = lax.axis_index('rows')
    me = lax.axis_index('states')
    zy = me // nx
    x = me % nx
    z = zy // ny
    y = zy % ny
    offsets = [(j, i) for j in range(nz) for i in range(ny)]
    rel = {o: k for k, o in enumerate(offsets)}
    mirror = [rel[(-j) % nz, (-i) % ny] for j, i in offsets]
    far = sorted(range(1, plane), key=lambda k: -(ring_distance(offsets[k][0], nz) + ring_distance(offsets[k][1], ny)))
    far_x = sorted(range(1, nx), key=lambda d: -ring_distance(d, nx))

    def plane_zy(k):
        return ((z + offsets[k][0]) % nz) * ny + (y + offsets[k][1]) % ny

    def plane_peer(k):
        return plane_zy(k) * nx + x

    def line_peer(d):
        return zy * nx + (x + d) % nx

    def remote(src, dst, send, recv, state, to=1):
        return pltpu.make_async_remote_copy(src_ref=src, dst_ref=dst, send_sem=send, recv_sem=recv,
                                            device_id={'rows': to, 'states': state},
                                            device_id_type=pl.DeviceIdType.MESH)

    def wait_bytes(ref, sem):
        pltpu.make_async_copy(ref, ref, sem).wait()

    def hand_over(h):
        return [remote(a_ref.at[pl.ds(plane_zy(k) * half, half)], a_loc.at[mirror[k], pl.ds(h * half, half)],
                       a_send.at[k], a_sem.at[mirror[k], h], plane_peer(k))
                for k in far + ([0] if h == 0 else [])]

    @pl.when(core == 0)
    def helper():
        first = remote(r0_ref, r_in.at[0, x, 0], r0_send, r0_sem, me)
        first.start()
        mine = pltpu.make_async_copy(e_ref, e_both.at[:, pl.ds(0, SB)], own_sem.at[0])
        mine.start()
        copies = hand_over(0)
        for copy in copies:
            copy.start()
        mine.wait()
        wait_bytes(e_both.at[:, pl.ds(SB, SB)], e_pair)

        def send_block(b, carry):
            src = e_both.at[pl.ds(b * rows, rows)]
            for k in [0] + far:
                remote(src, e_loc.at[b, mirror[k]], e_send, e_sem.at[b], plane_peer(k)).start()
            wait_bytes(e_loc.at[b], e_send)
            return carry

        lax.fori_loop(0, n_blocks, send_block, 0)
        first.wait_send()
        for copy in copies:
            copy.wait_send()
        wait_bytes(fin_alpha, f_recv.at[0])
        wait_bytes(fin_ll, f_recv.at[1])
        alpha_ref[...] = fin_alpha[...]
        ll_ref[...] = fin_ll[...]

    @pl.when(core == 1)
    def owner():
        eye = (lax.broadcasted_iota(jnp.int32, (batch, SB), 0)
               == lax.broadcasted_iota(jnp.int32, (batch, SB), 1))

        def as_row(tile):
            col = jnp.sum(tile, axis=1, keepdims=True)
            return jnp.sum(jnp.where(eye, col, 0.0), axis=0, keepdims=True)

        def as_col(row):
            return jnp.sum(jnp.where(eye, row, 0.0), axis=1, keepdims=True)

        def start_gather(slot):
            for d in far_x:
                remote(r_in.at[slot, x], r_in.at[slot, x], g_send, g_recv.at[slot], line_peer(d)).start()

        def start_plane_sums(slot):
            for k in far:
                remote(p_in.at[slot, zy], p_in.at[slot, zy], p_send, p_recv.at[slot], plane_peer(k)).start()

        others = pl.ds(0, nx - 1)
        peers = pl.ds(0, plane - 1)

        def finish_norm(slot):
            wait_bytes(p_in.at[slot, peers], p_recv.at[slot])
            c_in[slot, x] = jnp.sum(p_in[slot], axis=0)
            for d in far_x:
                remote(c_in.at[slot, x], c_in.at[slot, x], c_send, c_recv.at[slot], line_peer(d)).start()

        def norm(slot):
            wait_bytes(c_in.at[slot, others], c_recv.at[slot])
            c_row = jnp.sum(c_in[slot], axis=0)
            return c_row, 1.0 / as_col(c_row)

        def keep(t, slot, c_row, inv):
            active = t < lencol_ref[...]
            for h in range(2):
                alpha_acc[h] = jnp.where(active, r_in[slot, x, h] * inv, alpha_acc[h])
            ll_acc[...] = ll_acc[...] + jnp.where(t < lenrow_ref[...], jnp.log(c_row * (1.0 / LIFT)), 0.0)

        def add_w(b, k, fresh):
            part = lax.dot_general(e_loc[b, k], a_loc[k], (((1,), (1,)), ((), ())), preferred_element_type=F32)
            slot = b % 2
            w_loc[slot] = jnp.where(fresh, 0.0, w_loc[slot]) + part

        copies = hand_over(1)
        pair = remote(e_ref, e_both.at[:, pl.ds(SB, SB)], own_sem.at[0], e_pair, me, to=0)
        pair.start()
        for copy in copies:
            copy.start()
        own = pltpu.make_async_copy(a_ref.at[pl.ds(zy * half, half)], a_loc.at[0, pl.ds(half, half)], own_sem.at[1])
        own.start()
        alpha_acc[...] = jnp.zeros_like(alpha_acc)
        ll_acc[...] = jnp.zeros_like(ll_acc)
        r_in[0, x, 1] = r0_ref[...]
        wait_bytes(r0_ref, r0_sem)
        p_in[0, zy] = as_row(r_in[0, x, 0] + r_in[0, x, 1])
        start_plane_sums(0)
        start_gather(0)
        finish_norm(0)
        wait_bytes(p_in.at[0, peers], p_send)
        own.wait()
        for k in range(plane):
            for h in range(2):
                if h == 0 or k:
                    wait_bytes(a_loc.at[k, pl.ds(h * half, half)], a_sem.at[k, h])
        pair.wait_send()
        for copy in copies:
            copy.wait_send()
        wait_bytes(e_loc.at[0], e_sem.at[0])
        w_loc[...] = jnp.zeros_like(w_loc)

        def first_w(k, carry):
            add_w(0, k, False)
            return carry

        lax.fori_loop(0, plane, first_w, 0)

        def one_step(t, carry):
            cur = t % 2
            nxt = (t + 1) % 2
            b = t // block
            row = pl.ds((t % block) * batch, batch)
            c_row, inv = norm(cur)
            wait_bytes(r_in.at[cur, others], g_recv.at[cur])
            total = jnp.zeros((batch, SB), F32)
            for h in range(2):
                for src in range(nx):
                    cols = pl.ds(h * half + src * SB, SB)
                    tile = (r_in[cur, src, h] * inv).astype(BF16)
                    a_bf[:, cols] = tile
                    total = total + tile.astype(F32) * w_loc[b % 2, row, cols]
            for i, k in enumerate(far + [0]):
                part = jnp.dot(a_bf[...], a_loc[k], preferred_element_type=F32)
                parts = (part[:, :SB], part[:, SB:])
                if k:
                    for h in range(2):
                        u_out[k - 1, h] = parts[h]
                    remote(u_out.at[k - 1], u_in.at[nxt, mirror[k] - 1], u_send, u_recv.at[nxt], plane_peer(k)).start()
                if i == 0:
                    p_in[nxt, zy] = as_row(total)
                    start_plane_sums(nxt)
            wait_bytes(r_in.at[cur, others], g_send)
            wait_bytes(c_in.at[cur, others], c_send)
            keep(t, cur, c_row, inv)
            wait_bytes(u_in.at[nxt], u_recv.at[nxt])
            for h in range(2):
                u = parts[h]
                for k in range(plane - 1):
                    u = u + u_in[nxt, k, h]
                r_in[nxt, x, h] = u * e_loc[b, 0, row, pl.ds(h * SB, SB)].astype(F32)
            start_gather(nxt)
            finish_norm(nxt)

            @pl.when(b + 1 < n_blocks)
            def next_w():
                k = t % block
                later = b + 1

                @pl.when(k == 0)
                def arrived():
                    wait_bytes(e_loc.at[later], e_sem.at[later])

                add_w(later, k, k == 0)

            wait_bytes(u_out, u_send)
            wait_bytes(p_in.at[nxt, peers], p_send)
            return carry

        lax.fori_loop(0, n_steps - 1, one_step, 0)
        last = (n_steps - 1) % 2
        c_row, inv = norm(last)
        wait_bytes(r_in.at[last, others], g_recv.at[last])
        keep(n_steps - 1, last, c_row, inv)
        wait_bytes(r_in.at[last, others], g_send)
        wait_bytes(c_in.at[last, others], c_send)
        result = [remote(alpha_acc.at[0], fin_alpha, f_send.at[0], f_recv.at[0], me, to=0),
                  remote(ll_acc, fin_ll, f_send.at[1], f_recv.at[1], me, to=0)]
        for copy in result:
            copy.start()
        alpha_ref[...] = alpha_acc[1]
        ll_ref[...] = ll_acc[...]
        for copy in result:
            copy.wait_send()


def solution(mesh):
    vec_axes = ('rows', 'states')
    nz, ny, nx = CHIPS
    plane = nz * ny

    def local_forward(trans_blk, emit_blk, init_blk, tokens, lengths):
        batch, n_steps = tokens.shape
        cols = 2 * SB
        a_blk = trans_blk.reshape(trans_blk.shape[0], cols)
        emis = jnp.transpose(jnp.take(emit_blk, jnp.roll(tokens, -1, axis=1), axis=1), (2, 1, 0))
        emis = emis * jnp.asarray(LIFT, emis.dtype)
        first_raw = init_blk[None, :] * emis[-1].astype(F32)
        len_col = jnp.broadcast_to(lengths[:, None], (batch, SB))
        len_row = jnp.pad(lengths, (0, SB - batch))[None, :]
        vmem = pl.BlockSpec(memory_space=pltpu.VMEM)
        hbm = pl.BlockSpec(memory_space=pl.ANY)
        dma = pltpu.SemaphoreType.DMA
        k_rows = 2 * nx * SB
        block_rows = plane * batch
        n_blocks = n_steps // plane
        alpha, ll = pl.pallas_call(
            functools.partial(forward_kernel, CHIPS, n_steps),
            out_shape=(jax.ShapeDtypeStruct((batch, SB), F32), jax.ShapeDtypeStruct((1, SB), F32)),
            in_specs=[hbm, hbm, vmem, vmem, vmem],
            out_specs=(vmem, vmem),
            scratch_shapes=[
                pltpu.VMEM((plane, k_rows, cols), BF16),
                pltpu.VMEM((n_steps * batch, cols), BF16),
                pltpu.VMEM((n_blocks, plane, block_rows, cols), BF16),
                pltpu.VMEM((2, block_rows, k_rows), F32),
                pltpu.VMEM((2, nx, 2, batch, SB), F32),
                pltpu.VMEM((2, nx, 1, SB), F32),
                pltpu.VMEM((2, plane, 1, SB), F32),
                pltpu.VMEM((2, plane - 1, 2, batch, SB), F32),
                pltpu.VMEM((plane - 1, 2, batch, SB), F32),
                pltpu.VMEM((batch, k_rows), BF16),
                pltpu.VMEM((2, batch, SB), F32),
                pltpu.VMEM((1, SB), F32),
                pltpu.VMEM((batch, SB), F32),
                pltpu.VMEM((1, SB), F32),
                dma((plane, 2)), dma((plane,)), dma, dma, dma((n_blocks,)), dma, dma, dma((2,)),
                dma((2,)), dma, dma((2,)), dma, dma((2,)), dma, dma((2,)), dma, dma((2,)), dma((2,)),
            ],
            compiler_params=pltpu.CompilerParams(has_side_effects=True, vmem_limit_bytes=48 * 1024 * 1024),
            cost_estimate=pl.CostEstimate(flops=2 * batch * (n_steps - 1) * plane * k_rows * cols,
                                          bytes_accessed=plane * k_rows * cols * 2, transcendentals=0),
        )(a_blk, emis.reshape(n_steps * batch, SB), first_raw, len_col, len_row)
        return ll[0, :batch], alpha

    return jax.shard_map(local_forward, mesh=mesh, in_specs=(P('rows', None, 'states'), P(vec_axes, None), P(vec_axes), P('seqs', None), P('seqs')), out_specs=(P('seqs'), P('seqs', vec_axes)), check_vma=False)
```

time: 1300 us -> 1290 us (level)
  no operation moved by 1% of the time
where the time goes in v2:
time: 1290 us
  Pallas kernels  1280 us (99%)
  local copies, waits for them, and re-layouts  13.2 us (1%)
    pallas_call x1, Pallas kernels, local_forward(): pl.pallas_call(functools.partial(forward_kernel, CHIPS, n_steps), out_sha...  1280 us

profile of v2, /device:TPU:1, one launch (start us, length us, event | category | flops | bytes accessed | tf_op | source)
XLA Modules:
  0.0 1293.8 jit_solution(4603424432715115559)
XLA Ops:
  0.6 0.0 copy-start
  0.6 0.0 copy-start.1
  0.7 0.8 pad_bitcast_fusion.lenrow_ref
  1.5 0.7 broadcast_in_dim.25.lencol_ref
  2.2 0.7 fusion.4
  2.9 0.8 fusion.3
  3.7 0.1 and_bitcast_fusion
  3.7 0.1 fusion.2
  3.8 0.1 copy.9
  3.9 0.0 copy-done
  4.0 6.2 gather_fusion
  10.1 0.4 fusion
  10.6 0.0 copy-done.1
  10.6 2.7 copy.15
  13.3 1279.4 %shard_map.68 = (f32[16,128]{1,0:T(8,128)S(1)}, f32[1,128]{1,0:T(1,128)S(1)}) custom-call(bf16[8192,256]{1,0:T(8,128)(2,1)S(1)} %bitcast.29, bf16[2048,128]{1,0:T(8,128)(2,1)S(1)} %bitcast.30, f32[16,128]{1,0:T(8,128)S(1)} %convert_multiply_fusion.r0_ref, s32[16,128]{1,0:T(8,128)S(1)} %broadcast_in_dim.25.lencol_ref, s32[1,128]{1,0:T(1,128)S(1)} %pad_bitcast_fusion.lenrow_ref), custom_call_target="tpu_custom_call" | custom-call | flops 17045651456 | bytes 8388608 | tf_op jit(solution)/shard_map/pallas_call | solution.py:260
  1292.7 0.5 slice_bitcast_fusion.1
  1293.2 0.6 copy.17
  (1 shorter events, 0.0 us)
Async XLA Ops:
  0.6 3.3 copy-start
  0.6 9.9 copy-start.1

commit v3 on v2

--- a/solution.py
+++ b/solution.py
@@ -10,6 +10,7 @@
 CHIPS = (4, 4, 4)
 SB = 128
 LIFT = 2.0 ** 64
+LAG = 3
 F32 = jnp.float32
 BF16 = jnp.bfloat16
 
@@ -183,22 +184,30 @@
                     tile = (r_in[cur, src, h] * inv).astype(BF16)
                     a_bf[:, cols] = tile
                     total = total + tile.astype(F32) * w_loc[b % 2, row, cols]
+            ready = []
+
+            def send_sum():
+                k, part = ready.pop(0)
+                for h in range(2):
+                    u_out[k - 1, h] = part[:, h * SB:(h + 1) * SB]
+                remote(u_out.at[k - 1], u_in.at[nxt, mirror[k] - 1], u_send, u_recv.at[nxt], plane_peer(k)).start()
+
             for i, k in enumerate(far + [0]):
-                part = jnp.dot(a_bf[...], a_loc[k], preferred_element_type=F32)
-                parts = (part[:, :SB], part[:, SB:])
-                if k:
-                    for h in range(2):
-                        u_out[k - 1, h] = parts[h]
-                    remote(u_out.at[k - 1], u_in.at[nxt, mirror[k] - 1], u_send, u_recv.at[nxt], plane_peer(k)).start()
-                if i == 0:
+                ready.append((k, jnp.dot(a_bf[...], a_loc[k], preferred_element_type=F32)))
+                if len(ready) > LAG:
+                    send_sum()
+                if i == 4:
                     p_in[nxt, zy] = as_row(total)
                     start_plane_sums(nxt)
+            while len(ready) > 1:
+                send_sum()
+            own_part = ready[0][1]
             wait_bytes(r_in.at[cur, others], g_send)
             wait_bytes(c_in.at[cur, others], c_send)
             keep(t, cur, c_row, inv)
             wait_bytes(u_in.at[nxt], u_recv.at[nxt])
             for h in range(2):
-                u = parts[h]
+                u = own_part[:, h * SB:(h + 1) * SB]
                 for k in range(plane - 1):
                     u = u + u_in[nxt, k, h]
                 r_in[nxt, x, h] = u * e_loc[b, 0, row, pl.ds(h * SB, SB)].astype(F32)

time: 1290 us -> 1150 us (0.89)
  Pallas kernels: 1280 us -> 1130 us
    pallas_call x1, Pallas kernels: 1280 us -> 1130 us  [local_forward(): pl.pallas_call(functools.partial(forward_kernel, CHIPS, n_steps), out_sha...]
where the time goes in v3:
time: 1150 us
  Pallas kernels  1130 us (98%)
  local copies, waits for them, and re-layouts  13.2 us (1%)
    pallas_call x1, Pallas kernels, local_forward(): pl.pallas_call(functools.partial(forward_kernel, CHIPS, n_steps), out_sha...  1130 us

profile of v3, /device:TPU:1, one launch (start us, length us, event | category | flops | bytes accessed | tf_op | source)
XLA Modules:
  0.0 1149.4 jit_solution(16459970517780408736)
XLA Ops:
  0.6 0.0 copy-start
  0.6 0.0 copy-start.1
  0.7 0.8 pad_bitcast_fusion.lenrow_ref
  1.5 0.7 broadcast_in_dim.25.lencol_ref
  2.2 0.7 fusion.4
  2.9 0.8 fusion.3
  3.7 0.1 and_bitcast_fusion
  3.7 0.1 fusion.2
  3.8 0.1 copy.9
  3.9 0.0 copy-done
  4.0 6.2 gather_fusion
  10.1 0.4 fusion
  10.6 0.0 copy-done.1
  10.6 2.7 copy.15
  13.3 1134.9 %shard_map.68 = (f32[16,128]{1,0:T(8,128)S(1)}, f32[1,128]{1,0:T(1,128)S(1)}) custom-call(bf16[8192,256]{1,0:T(8,128)(2,1)S(1)} %bitcast.29, bf16[2048,128]{1,0:T(8,128)(2,1)S(1)} %bitcast.30, f32[16,128]{1,0:T(8,128)S(1)} %convert_multiply_fusion.r0_ref, s32[16,128]{1,0:T(8,128)S(1)} %broadcast_in_dim.25.lencol_ref, s32[1,128]{1,0:T(1,128)S(1)} %pad_bitcast_fusion.lenrow_ref), custom_call_target="tpu_custom_call" | custom-call | flops 17045651456 | bytes 8388608 | tf_op jit(solution)/shard_map/pallas_call | solution.py:269
  1148.3 0.5 slice_bitcast_fusion.1
  1148.8 0.6 copy.17
  (1 shorter events, 0.0 us)
Async XLA Ops:
  0.6 3.3 copy-start
  0.6 9.9 copy-start.1

commit v4 on v3

--- a/solution.py
+++ b/solution.py
@@ -11,6 +11,7 @@
 SB = 128
 LIFT = 2.0 ** 64
 LAG = 3
+P_AFTER = 2
 F32 = jnp.float32
 BF16 = jnp.bfloat16
 
@@ -194,17 +195,18 @@
 
             for i, k in enumerate(far + [0]):
                 ready.append((k, jnp.dot(a_bf[...], a_loc[k], preferred_element_type=F32)))
+                if i == P_AFTER:
+                    p_in[nxt, zy] = as_row(total)
+                    start_plane_sums(nxt)
                 if len(ready) > LAG:
                     send_sum()
-                if i == 4:
-                    p_in[nxt, zy] = as_row(total)
-                    start_plane_sums(nxt)
             while len(ready) > 1:
                 send_sum()
             own_part = ready[0][1]
             wait_bytes(r_in.at[cur, others], g_send)
             wait_bytes(c_in.at[cur, others], c_send)
             keep(t, cur, c_row, inv)
+            finish_norm(nxt)
             wait_bytes(u_in.at[nxt], u_recv.at[nxt])
             for h in range(2):
                 u = own_part[:, h * SB:(h + 1) * SB]
@@ -212,7 +214,6 @@
                     u = u + u_in[nxt, k, h]
                 r_in[nxt, x, h] = u * e_loc[b, 0, row, pl.ds(h * SB, SB)].astype(F32)
             start_gather(nxt)
-            finish_norm(nxt)
 
             @pl.when(b + 1 < n_blocks)
             def next_w():

time: 1150 us -> 1110 us (0.965)
  Pallas kernels: 1130 us -> 1090 us
    pallas_call x1, Pallas kernels: 1130 us -> 1090 us  [local_forward(): pl.pallas_call(functools.partial(forward_kernel, CHIPS, n_steps), out_sha...]
where the time goes in v4:
time: 1110 us; the launch traced here: 1100 us
  Pallas kernels  1090 us (98%)
  local copies, waits for them, and re-layouts  13.2 us (1%)
    pallas_call x1, Pallas kernels, local_forward(): pl.pallas_call(functools.partial(forward_kernel, CHIPS, n_steps), out_sha...  1090 us

profile of v4, /device:TPU:1, one launch (start us, length us, event | category | flops | bytes accessed | tf_op | source)
XLA Modules:
  0.0 1102.4 jit_solution(6060373292607426107)
XLA Ops:
  0.6 0.0 copy-start
  0.6 0.0 copy-start.1
  0.7 0.8 pad_bitcast_fusion.lenrow_ref
  1.5 0.7 broadcast_in_dim.25.lencol_ref
  2.2 0.7 fusion.4
  2.9 0.8 fusion.3
  3.7 0.1 and_bitcast_fusion
  3.7 0.1 fusion.2
  3.8 0.1 copy.9
  3.9 0.0 copy-done
  4.0 6.2 gather_fusion
  10.1 0.4 fusion
  10.6 0.0 copy-done.1
  10.6 2.7 copy.15
  13.3 1087.9 %shard_map.68 = (f32[16,128]{1,0:T(8,128)S(1)}, f32[1,128]{1,0:T(1,128)S(1)}) custom-call(bf16[8192,256]{1,0:T(8,128)(2,1)S(1)} %bitcast.29, bf16[2048,128]{1,0:T(8,128)(2,1)S(1)} %bitcast.30, f32[16,128]{1,0:T(8,128)S(1)} %convert_multiply_fusion.r0_ref, s32[16,128]{1,0:T(8,128)S(1)} %broadcast_in_dim.25.lencol_ref, s32[1,128]{1,0:T(1,128)S(1)} %pad_bitcast_fusion.lenrow_ref), custom_call_target="tpu_custom_call" | custom-call | flops 17045651456 | bytes 8388608 | tf_op jit(solution)/shard_map/pallas_call | solution.py:270
  1101.3 0.5 slice_bitcast_fusion.1
  1101.8 0.6 copy.17
  (1 shorter events, 0.0 us)
Async XLA Ops:
  0.6 3.3 copy-start
  0.6 9.9 copy-start.1

commit v5 on v4

--- a/solution.py
+++ b/solution.py
@@ -12,6 +12,8 @@
 LIFT = 2.0 ** 64
 LAG = 3
 P_AFTER = 2
+BLOCK = 8
+AHEAD = 6
 F32 = jnp.float32
 BF16 = jnp.bfloat16
 
@@ -20,16 +22,16 @@
     return min(offset, n - offset)
 
 
-def forward_kernel(dims, n_steps, a_ref, e_ref, r0_ref, lencol_ref, lenrow_ref, alpha_ref, ll_ref,
-                   a_loc, e_both, e_loc, w_loc, r_in, c_in, p_in, u_in, u_out, a_bf, alpha_acc, ll_acc, fin_alpha,
-                   fin_ll, a_sem, a_send, e_pair, e_send, e_sem, r0_sem, r0_send, own_sem,
+def forward_kernel(dims, n_steps, block, a_ref, e_ref, r0_ref, len_ref, alpha_ref, ll_ref,
+                   a_loc, e_both, e_loc, w_loc, r_in, c_in, p_in, u_in, u_out, a_bf, len_col, alpha_acc, ll_acc, fin_alpha,
+                   fin_ll, tick, a_sem, a_send, e_pair, e_send, e_sem, r0_sem, r0_send, own_sem,
                    g_recv, g_send, c_recv, c_send, u_recv, u_send, p_recv, p_send, f_recv, f_send):
     nz, ny, nx = dims
     plane = nz * ny
     batch = r0_ref.shape[0]
     half = nx * SB
-    block = plane
     rows = block * batch
+    per_step = plane // block
     n_blocks = n_steps // block
     core = lax.axis_index('rows')
     me = lax.axis_index('states')
@@ -60,31 +62,53 @@
     def wait_bytes(ref, sem):
         pltpu.make_async_copy(ref, ref, sem).wait()
 
-    def hand_over(h):
-        return [remote(a_ref.at[pl.ds(plane_zy(k) * half, half)], a_loc.at[mirror[k], pl.ds(h * half, half)],
-                       a_send.at[k], a_sem.at[mirror[k], h], plane_peer(k))
-                for k in far + ([0] if h == 0 else [])]
+    def slot_peer(j):
+        return (((z - j // ny + nz) % nz) * ny + (y - j % ny + ny) % ny) * nx + x
+
+    def a_copy(h, j):
+        peer = slot_peer(j)
+        return remote(a_ref.at[pl.ds((peer // nx) * half, half)], a_loc.at[j, pl.ds(h * half, half)],
+                      a_send.at[j], a_sem.at[j, h], peer)
+
+    def e_copy(b, j):
+        return remote(e_both.at[pl.ds(b * rows, rows)], e_loc.at[b, j], e_send, e_sem.at[b % 2, j], slot_peer(j))
+
+    barrier = pltpu.get_barrier_semaphore()
+
+    def announce(state, to):
+        pl.semaphore_signal(barrier, inc=1, device_id={'rows': to, 'states': state}, device_id_type=pl.DeviceIdType.MESH)
 
     @pl.when(core == 0)
     def helper():
+        announce(me, 1)
+        pl.semaphore_wait(barrier, plane)
         first = remote(r0_ref, r_in.at[0, x, 0], r0_send, r0_sem, me)
         first.start()
         mine = pltpu.make_async_copy(e_ref, e_both.at[:, pl.ds(0, SB)], own_sem.at[0])
         mine.start()
-        copies = hand_over(0)
-        for copy in copies:
-            copy.start()
+        copies = [a_copy(0, j) for j in range(plane)]
+        copies[0].start()
+        copies[1].start()
         mine.wait()
         wait_bytes(e_both.at[:, pl.ds(SB, SB)], e_pair)
-
-        def send_block(b, carry):
-            src = e_both.at[pl.ds(b * rows, rows)]
-            for k in [0] + far:
-                remote(src, e_loc.at[b, mirror[k]], e_send, e_sem.at[b], plane_peer(k)).start()
-            wait_bytes(e_loc.at[b], e_send)
+        e_copy(0, 0).start()
+        e_copy(0, 1).start()
+        for j in range(2, plane):
+            copies[j].start()
+            e_copy(0, j).start()
+        wait_bytes(e_loc.at[0], e_send)
+
+        def send_part(i, carry):
+            @pl.when(i >= AHEAD)
+            def paced():
+                pl.semaphore_wait(tick, 1)
+
+            for n in range(per_step):
+                e_copy(1 + i // block, (i % block) * per_step + n).start()
+            wait_bytes(e_loc.at[0, pl.ds(0, per_step)], e_send)
             return carry
 
-        lax.fori_loop(0, n_blocks, send_block, 0)
+        lax.fori_loop(0, n_steps - block, send_part, 0)
         first.wait_send()
         for copy in copies:
             copy.wait_send()
@@ -128,25 +152,35 @@
             return c_row, 1.0 / as_col(c_row)
 
         def keep(t, slot, c_row, inv):
-            active = t < lencol_ref[...]
+            now = lax.convert_element_type(t, F32)
+            active = now < len_col[...]
             for h in range(2):
                 alpha_acc[h] = jnp.where(active, r_in[slot, x, h] * inv, alpha_acc[h])
-            ll_acc[...] = ll_acc[...] + jnp.where(t < lenrow_ref[...], jnp.log(c_row * (1.0 / LIFT)), 0.0)
+            ll_acc[...] = ll_acc[...] + jnp.where(now < len_ref[...], jnp.log(c_row * (1.0 / LIFT)), 0.0)
 
         def add_w(b, k, fresh):
             part = lax.dot_general(e_loc[b, k], a_loc[k], (((1,), (1,)), ((), ())), preferred_element_type=F32)
             slot = b % 2
             w_loc[slot] = jnp.where(fresh, 0.0, w_loc[slot]) + part
 
-        copies = hand_over(1)
+        for k in far:
+            announce(plane_peer(k), 1)
+        for d in far_x:
+            announce(line_peer(d), 1)
+        for k in range(plane):
+            announce(plane_peer(k), 0)
+        pl.semaphore_wait(barrier, plane + nx - 1)
         pair = remote(e_ref, e_both.at[:, pl.ds(SB, SB)], own_sem.at[0], e_pair, me, to=0)
         pair.start()
+        copies = [a_copy(1, j) for j in range(1, plane)]
         for copy in copies:
             copy.start()
         own = pltpu.make_async_copy(a_ref.at[pl.ds(zy * half, half)], a_loc.at[0, pl.ds(half, half)], own_sem.at[1])
         own.start()
         alpha_acc[...] = jnp.zeros_like(alpha_acc)
         ll_acc[...] = jnp.zeros_like(ll_acc)
+        w_loc[...] = jnp.zeros_like(w_loc)
+        len_col[...] = jnp.broadcast_to(as_col(len_ref[...]), (batch, SB))
         r_in[0, x, 1] = r0_ref[...]
         wait_bytes(r0_ref, r0_sem)
         p_in[0, zy] = as_row(r_in[0, x, 0] + r_in[0, x, 1])
@@ -155,21 +189,22 @@
         finish_norm(0)
         wait_bytes(p_in.at[0, peers], p_send)
         own.wait()
-        for k in range(plane):
-            for h in range(2):
-                if h == 0 or k:
-                    wait_bytes(a_loc.at[k, pl.ds(h * half, half)], a_sem.at[k, h])
+
+        def first_w(k, carry):
+            wait_bytes(a_loc.at[k, pl.ds(0, half)], a_sem.at[k, 0])
+
+            @pl.when(k > 0)
+            def from_owner():
+                wait_bytes(a_loc.at[k, pl.ds(half, half)], a_sem.at[k, 1])
+
+            wait_bytes(e_loc.at[0, k], e_sem.at[0, k])
+            add_w(0, k, False)
+            return carry
+
+        lax.fori_loop(0, plane, first_w, 0)
         pair.wait_send()
         for copy in copies:
             copy.wait_send()
-        wait_bytes(e_loc.at[0], e_sem.at[0])
-        w_loc[...] = jnp.zeros_like(w_loc)
-
-        def first_w(k, carry):
-            add_w(0, k, False)
-            return carry
-
-        lax.fori_loop(0, plane, first_w, 0)
 
         def one_step(t, carry):
             cur = t % 2
@@ -215,16 +250,18 @@
                 r_in[nxt, x, h] = u * e_loc[b, 0, row, pl.ds(h * SB, SB)].astype(F32)
             start_gather(nxt)
 
+            @pl.when(t < n_steps - block - AHEAD)
+            def go_on():
+                pl.semaphore_signal(tick, inc=1, device_id={'rows': 0, 'states': me},
+                                    device_id_type=pl.DeviceIdType.MESH)
+
             @pl.when(b + 1 < n_blocks)
             def next_w():
-                k = t % block
                 later = b + 1
-
-                @pl.when(k == 0)
-                def arrived():
-                    wait_bytes(e_loc.at[later], e_sem.at[later])
-
-                add_w(later, k, k == 0)
+                for n in range(per_step):
+                    k = (t % block) * per_step + n
+                    wait_bytes(e_loc.at[later, k], e_sem.at[later % 2, k])
+                    add_w(later, k, k == 0)
 
             wait_bytes(u_out, u_send)
             wait_bytes(p_in.at[nxt, peers], p_send)
@@ -256,21 +293,21 @@
         batch, n_steps = tokens.shape
         cols = 2 * SB
         a_blk = trans_blk.reshape(trans_blk.shape[0], cols)
-        emis = jnp.transpose(jnp.take(emit_blk, jnp.roll(tokens, -1, axis=1), axis=1), (2, 1, 0))
+        emis = jnp.transpose(emit_blk.at[:, jnp.roll(tokens, -1, axis=1)].get(mode='promise_in_bounds'), (2, 1, 0))
         emis = emis * jnp.asarray(LIFT, emis.dtype)
         first_raw = init_blk[None, :] * emis[-1].astype(F32)
-        len_col = jnp.broadcast_to(lengths[:, None], (batch, SB))
-        len_row = jnp.pad(lengths, (0, SB - batch))[None, :]
+        len_row = jnp.pad(lengths.astype(F32), (0, SB - batch))[None, :]
         vmem = pl.BlockSpec(memory_space=pltpu.VMEM)
         hbm = pl.BlockSpec(memory_space=pl.ANY)
         dma = pltpu.SemaphoreType.DMA
         k_rows = 2 * nx * SB
-        block_rows = plane * batch
-        n_blocks = n_steps // plane
+        block = min(BLOCK, plane)
+        block_rows = block * batch
+        n_blocks = n_steps // block
         alpha, ll = pl.pallas_call(
-            functools.partial(forward_kernel, CHIPS, n_steps),
+            functools.partial(forward_kernel, CHIPS, n_steps, block),
             out_shape=(jax.ShapeDtypeStruct((batch, SB), F32), jax.ShapeDtypeStruct((1, SB), F32)),
-            in_specs=[hbm, hbm, vmem, vmem, vmem],
+            in_specs=[hbm, hbm, vmem, vmem],
             out_specs=(vmem, vmem),
             scratch_shapes=[
                 pltpu.VMEM((plane, k_rows, cols), BF16),
@@ -283,17 +320,19 @@
                 pltpu.VMEM((2, plane - 1, 2, batch, SB), F32),
                 pltpu.VMEM((plane - 1, 2, batch, SB), F32),
                 pltpu.VMEM((batch, k_rows), BF16),
+                pltpu.VMEM((batch, SB), F32),
                 pltpu.VMEM((2, batch, SB), F32),
                 pltpu.VMEM((1, SB), F32),
                 pltpu.VMEM((batch, SB), F32),
                 pltpu.VMEM((1, SB), F32),
-                dma((plane, 2)), dma((plane,)), dma, dma, dma((n_blocks,)), dma, dma, dma((2,)),
+                pltpu.SemaphoreType.REGULAR,
+                dma((plane, 2)), dma((plane,)), dma, dma, dma((2, plane)), dma, dma, dma((2,)),
                 dma((2,)), dma, dma((2,)), dma, dma((2,)), dma, dma((2,)), dma, dma((2,)), dma((2,)),
             ],
-            compiler_params=pltpu.CompilerParams(has_side_effects=True, vmem_limit_bytes=48 * 1024 * 1024),
+            compiler_params=pltpu.CompilerParams(collective_id=0, has_side_effects=True, vmem_limit_bytes=48 * 1024 * 1024),
             cost_estimate=pl.CostEstimate(flops=2 * batch * (n_steps - 1) * plane * k_rows * cols,
                                           bytes_accessed=plane * k_rows * cols * 2, transcendentals=0),
-        )(a_blk, emis.reshape(n_steps * batch, SB), first_raw, len_col, len_row)
+        )(a_blk, emis.reshape(n_steps * batch, SB), first_raw, len_row)
         return ll[0, :batch], alpha
 
     return jax.shard_map(local_forward, mesh=mesh, in_specs=(P('rows', None, 'states'), P(vec_axes, None), P(vec_axes), P('seqs', None), P('seqs')), out_specs=(P('seqs'), P('seqs', vec_axes)), check_vma=False)

time: 1110 us -> 1060 us (0.955)
  Pallas kernels: 1090 us -> 1050 us
    pallas_call x1, Pallas kernels: 1090 us -> 1050 us  [local_forward(): pl.pallas_call(functools.partial(forward_kernel, CHIPS, n_steps, block),...]
where the time goes in v5:
time: 1060 us
  Pallas kernels  1050 us (99%)
  local copies, waits for them, and re-layouts  11.9 us (1%)
    pallas_call x1, Pallas kernels, local_forward(): pl.pallas_call(functools.partial(forward_kernel, CHIPS, n_steps, block),...  1050 us

profile of v5, /device:TPU:1, one launch (start us, length us, event | category | flops | bytes accessed | tf_op | source)
XLA Modules:
  0.0 1061.5 jit_solution(7003862894550582713)
XLA Ops:
  0.6 0.0 copy-start
  0.6 0.0 copy-start.1
  0.7 0.8 convert_element_type.13
  1.5 0.7 slice_bitcast_fusion
  2.2 0.8 slice_bitcast_fusion.1
  2.9 0.1 fusion.1
  3.0 0.0 copy-done
  3.0 6.2 gather_fusion
  9.3 0.3 copy.15
  9.6 0.0 copy-done.1
  9.6 2.7 copy.14
  12.4 1048.0 %shard_map.68 = (f32[16,128]{1,0:T(8,128)S(1)}, f32[1,128]{1,0:T(1,128)S(1)}) custom-call(bf16[8192,256]{1,0:T(8,128)(2,1)S(1)} %bitcast.27, bf16[2048,128]{1,0:T(8,128)(2,1)S(1)} %bitcast.29, f32[16,128]{1,0:T(8,128)S(1)} %convert_multiply_fusion.r0_ref, f32[1,128]{1,0:T(1,128)S(1)} %pad_bitcast_fusion.len_ref), custom_call_target="tpu_custom_call" | custom-call | flops 17045651456 | bytes 8388608 | tf_op jit(solution)/shard_map/pallas_call | solution.py:307
  1060.4 0.5 slice_bitcast_fusion.3
  1060.9 0.6 copy.17
  (3 shorter events, 0.1 us)
Async XLA Ops:
  0.6 2.4 copy-start
  0.6 9.0 copy-start.1

commit v6 on v5

v6 whole, which is shorter than its diff:
```python
import functools

import jax
import jax.numpy as jnp
from jax import lax
from jax.experimental import pallas as pl
from jax.experimental.pallas import tpu as pltpu
from jax.sharding import PartitionSpec as P

CHIPS = (4, 4, 4)
SB = 128
LIFT = 2.0 ** 64
LAG = 1
P_AFTER = 1
BLOCK = 8
AHEAD = 6
F32 = jnp.float32
BF16 = jnp.bfloat16


def ring_distance(offset, n):
    return min(offset, n - offset)


def forward_kernel(dims, n_steps, block, a_ref, e_ref, r0_ref, len_ref, alpha_ref, ll_ref,
                   a_loc, e_both, e_loc, w_loc, r_in, c_in, p_in, u_in, u_out, a_bf, len_col, alpha_acc, ll_acc,
                   fin_alpha, fin_ll, tick, a_sem, a_send, e_pair, e_send, e_sem, r0_sem, r0_send, own_sem,
                   g_recv, g_send, c_recv, c_send, u_recv, u_send, p_recv, p_send, f_recv, f_send):
    nz, ny, nx = dims
    n_sum, n_gather = 2 * nz, 2 * nx
    batch = r0_ref.shape[0]
    half = n_gather * SB
    rows = block * batch
    n_blocks = n_steps // block
    per_step = n_sum // block
    core = lax.axis_index('rows')
    me = lax.axis_index('states')
    z = me // (ny * nx)
    y = (me // nx) % ny
    x = me % nx
    group = me // n_gather
    place = me % n_gather
    c_place = (((y + 1) // 2) % 2) * nx + x
    far = sorted(range(1, n_sum), key=lambda k: -(ring_distance(k // 2, nz) + k % 2))
    far_gather = sorted(((f, d) for f in range(2) for d in range(nx) if f or d),
                        key=lambda o: -(o[0] + ring_distance(o[1], nx)))

    def sum_peer(k, sign=1):
        flip = k % 2
        return ((z + sign * (k // 2) + nz) % nz) * ny * nx + (y + flip * (ny - 1 - 2 * y)) * nx + x

    def mirror(k):
        return ((nz - k // 2) % nz) * 2 + k % 2

    def gather_peer(flip, d):
        return (me // (ny * nx)) * ny * nx + (y + flip * (1 - 2 * (y % 2))) * nx + (x + d) % nx

    def remote(src, dst, send, recv, state, to=1):
        return pltpu.make_async_remote_copy(src_ref=src, dst_ref=dst, send_sem=send, recv_sem=recv,
                                            device_id={'rows': to, 'states': state},
                                            device_id_type=pl.DeviceIdType.MESH)

    def wait_bytes(ref, sem):
        pltpu.make_async_copy(ref, ref, sem).wait()

    def a_copy(h, k):
        peer = sum_peer(k, -1)
        return remote(a_ref.at[pl.ds((peer // n_gather) * half, half)], a_loc.at[k, pl.ds(h * half, half)],
                      a_send.at[k], a_sem.at[k, h], peer)

    def e_copy(b, k):
        return remote(e_both.at[pl.ds(b * rows, rows)], e_loc.at[b, k], e_send, e_sem.at[b % 2, k], sum_peer(k, -1))

    barrier = pltpu.get_barrier_semaphore()

    def announce(state, to):
        pl.semaphore_signal(barrier, inc=1, device_id={'rows': to, 'states': state}, device_id_type=pl.DeviceIdType.MESH)

    @pl.when(core == 0)
    def helper():
        announce(me, 1)
        pl.semaphore_wait(barrier, n_sum)
        first = remote(r0_ref, r_in.at[0, place, 0], r0_send, r0_sem, me)
        first.start()
        mine = pltpu.make_async_copy(e_ref, e_both.at[:, pl.ds(0, SB)], own_sem.at[0])
        mine.start()
        copies = [a_copy(0, k) for k in range(n_sum)]
        copies[0].start()
        copies[1].start()
        mine.wait()
        wait_bytes(e_both.at[:, pl.ds(SB, SB)], e_pair)
        e_copy(0, 0).start()
        e_copy(0, 1).start()
        for k in range(2, n_sum):
            copies[k].start()
            e_copy(0, k).start()
        wait_bytes(e_loc.at[0], e_send)

        def send_part(i, carry):
            @pl.when(i >= AHEAD)
            def paced():
                pl.semaphore_wait(tick, 1)

            for n in range(per_step):
                e_copy(1 + i // block, (i % block) * per_step + n).start()
            wait_bytes(e_loc.at[0, pl.ds(0, per_step)], e_send)
            return carry

        lax.fori_loop(0, n_steps - block, send_part, 0)
        first.wait_send()
        for copy in copies:
            copy.wait_send()
        wait_bytes(fin_alpha, f_recv.at[0])
        wait_bytes(fin_ll, f_recv.at[1])
        alpha_ref[...] = fin_alpha[...]
        ll_ref[...] = fin_ll[...]

    @pl.when(core == 1)
    def owner():
        eye = (lax.broadcasted_iota(jnp.int32, (batch, SB), 0)
               == lax.broadcasted_iota(jnp.int32, (batch, SB), 1))

        def as_row(tile):
            col = jnp.sum(tile, axis=1, keepdims=True)
            return jnp.sum(jnp.where(eye, col, 0.0), axis=0, keepdims=True)

        def as_col(row):
            return jnp.sum(jnp.where(eye, row, 0.0), axis=1, keepdims=True)

        def start_gather(slot):
            for o in far_gather:
                remote(r_in.at[slot, place], r_in.at[slot, place], g_send, g_recv.at[slot], gather_peer(*o)).start()

        def start_parts(slot):
            for k in far:
                remote(p_in.at[slot, group], p_in.at[slot, group], p_send, p_recv.at[slot], sum_peer(k)).start()

        others = pl.ds(0, n_gather - 1)
        peers = pl.ds(0, n_sum - 1)

        def finish_norm(slot):
            wait_bytes(p_in.at[slot, peers], p_recv.at[slot])
            c_in[slot, c_place] = jnp.sum(p_in[slot], axis=0)
            for o in far_gather:
                remote(c_in.at[slot, c_place], c_in.at[slot, c_place], c_send, c_recv.at[slot], gather_peer(*o)).start()

        def norm(slot):
            wait_bytes(c_in.at[slot, others], c_recv.at[slot])
            c_row = jnp.sum(c_in[slot], axis=0)
            c_col = as_col(c_row)
            inv = 1.0 / c_col
            return c_row, inv * (2.0 - c_col * inv)

        def keep(t, slot, c_row, inv):
            now = lax.convert_element_type(t, F32)
            active = now < len_col[...]
            for h in range(2):
                alpha_acc[h] = jnp.where(active, r_in[slot, place, h] * inv, alpha_acc[h])
            ll_acc[...] = ll_acc[...] + jnp.where(now < len_ref[...], jnp.log(c_row * (1.0 / LIFT)), 0.0)

        def add_w(b, k, fresh):
            part = lax.dot_general(e_loc[b, k], a_loc[k], (((1,), (1,)), ((), ())), preferred_element_type=F32)
            slot = b % 2
            w_loc[slot] = jnp.where(fresh, 0.0, w_loc[slot]) + part

        for k in far:
            announce(sum_peer(k), 1)
        for o in far_gather:
            announce(gather_peer(*o), 1)
        for k in range(n_sum):
            announce(sum_peer(k), 0)
        pl.semaphore_wait(barrier, n_sum + n_gather - 1)
        pair = remote(e_ref, e_both.at[:, pl.ds(SB, SB)], own_sem.at[0], e_pair, me, to=0)
        pair.start()
        copies = [a_copy(1, k) for k in range(1, n_sum)]
        for copy in copies:
            copy.start()
        own = pltpu.make_async_copy(a_ref.at[pl.ds(group * half, half)], a_loc.at[0, pl.ds(half, half)], own_sem.at[1])
        own.start()
        alpha_acc[...] = jnp.zeros_like(alpha_acc)
        ll_acc[...] = jnp.zeros_like(ll_acc)
        w_loc[...] = jnp.zeros_like(w_loc)
        len_col[...] = jnp.broadcast_to(as_col(len_ref[...]), (batch, SB))
        r_in[0, place, 1] = r0_ref[...]
        wait_bytes(r0_ref, r0_sem)
        p_in[0, group] = as_row(r_in[0, place, 0] + r_in[0, place, 1])
        start_parts(0)
        start_gather(0)
        finish_norm(0)
        wait_bytes(p_in.at[0, peers], p_send)
        own.wait()

        def first_w(k, carry):
            wait_bytes(a_loc.at[k, pl.ds(0, half)], a_sem.at[k, 0])

            @pl.when(k > 0)
            def from_owner():
                wait_bytes(a_loc.at[k, pl.ds(half, half)], a_sem.at[k, 1])

            wait_bytes(e_loc.at[0, k], e_sem.at[0, k])
            add_w(0, k, False)
            return carry

        lax.fori_loop(0, n_sum, first_w, 0)
        pair.wait_send()
        for copy in copies:
            copy.wait_send()

        def one_step(t, carry):
            cur = t % 2
            nxt = (t + 1) % 2
            b = t // block
            row = pl.ds((t % block) * batch, batch)
            c_row, inv = norm(cur)
            wait_bytes(r_in.at[cur, others], g_recv.at[cur])
            total = jnp.zeros((batch, SB), F32)
            for h in range(2):
                for src in range(n_gather):
                    cols = pl.ds(h * half + src * SB, SB)
                    tile = (r_in[cur, src, h] * inv).astype(BF16)
                    a_bf[:, cols] = tile
                    total = total + tile.astype(F32) * w_loc[b % 2, row, cols]
            unit = jnp.where(t >= 0, jnp.float32(1.0), jnp.float32(0.0))
            ready = []

            def send_sum():
                k, part = ready.pop(0)
                for h in range(2):
                    u_out[k - 1, h] = part[:, h * SB:(h + 1) * SB]
                remote(u_out.at[k - 1], u_in.at[nxt, mirror(k) - 1], u_send, u_recv.at[nxt], sum_peer(k)).start()

            for i, k in enumerate(far + [0]):
                low = jnp.dot(a_bf[:, :half], a_loc[k, :half], preferred_element_type=F32)
                high = jnp.dot(a_bf[:, half:], a_loc[k, half:], preferred_element_type=F32)
                ready.append((k, low * unit + high))
                if i == P_AFTER:
                    p_in[nxt, group] = as_row(total)
                    start_parts(nxt)
                if len(ready) > LAG:
                    send_sum()
            while len(ready) > 1:
                send_sum()
            own_part = ready[0][1]
            wait_bytes(r_in.at[cur, others], g_send)
            wait_bytes(c_in.at[cur, others], c_send)
            keep(t, cur, c_row, inv)
            finish_norm(nxt)
            wait_bytes(u_in.at[nxt], u_recv.at[nxt])
            for h in range(2):
                parts = [own_part[:, h * SB:(h + 1) * SB]] + [u_in[nxt, k, h] for k in range(n_sum - 1)]
                while len(parts) > 1:
                    parts = [parts[i] + parts[i + 1] for i in range(0, len(parts), 2)]
                r_in[nxt, place, h] = parts[0] * e_loc[b, 0, row, pl.ds(h * SB, SB)].astype(F32)
            start_gather(nxt)

            @pl.when(t < n_steps - block - AHEAD)
            def go_on():
                pl.semaphore_signal(tick, inc=1, device_id={'rows': 0, 'states': me},
                                    device_id_type=pl.DeviceIdType.MESH)

            @pl.when(b + 1 < n_blocks)
            def next_w():
                later = b + 1
                for n in range(per_step):
                    k = (t % block) * per_step + n
                    wait_bytes(e_loc.at[later, k], e_sem.at[later % 2, k])
                    add_w(later, k, k == 0)

            wait_bytes(u_out, u_send)
            wait_bytes(p_in.at[nxt, peers], p_send)
            return carry

        lax.fori_loop(0, n_steps - 1, one_step, 0)
        last = (n_steps - 1) % 2
        c_row, inv = norm(last)
        wait_bytes(r_in.at[last, others], g_recv.at[last])
        keep(n_steps - 1, last, c_row, inv)
        wait_bytes(r_in.at[last, others], g_send)
        wait_bytes(c_in.at[last, others], c_send)
        result = [remote(alpha_acc.at[0], fin_alpha, f_send.at[0], f_recv.at[0], me, to=0),
                  remote(ll_acc, fin_ll, f_send.at[1], f_recv.at[1], me, to=0)]
        for copy in result:
            copy.start()
        alpha_ref[...] = alpha_acc[1]
        ll_ref[...] = ll_acc[...]
        for copy in result:
            copy.wait_send()


def solution(mesh):
    vec_axes = ('rows', 'states')
    nz, ny, nx = CHIPS
    n_sum, n_gather = 2 * nz, 2 * nx

    def local_forward(trans_blk, emit_blk, init_blk, tokens, lengths):
        batch, n_steps = tokens.shape
        cols = 2 * SB
        a_blk = trans_blk.reshape(trans_blk.shape[0], cols)
        emis = jnp.transpose(emit_blk.at[:, jnp.roll(tokens, -1, axis=1)].get(mode='promise_in_bounds'), (2, 1, 0))
        emis = emis * jnp.asarray(LIFT, emis.dtype)
        first_raw = init_blk[None, :] * emis[-1].astype(F32)
        len_row = jnp.pad(lengths.astype(F32), (0, SB - batch))[None, :]
        vmem = pl.BlockSpec(memory_space=pltpu.VMEM)
        hbm = pl.BlockSpec(memory_space=pl.ANY)
        dma = pltpu.SemaphoreType.DMA
        k_rows = 2 * n_gather * SB
        block = min(BLOCK, n_sum)
        block_rows = block * batch
        n_blocks = n_steps // block
        alpha, ll = pl.pallas_call(
            functools.partial(forward_kernel, CHIPS, n_steps, block),
            out_shape=(jax.ShapeDtypeStruct((batch, SB), F32), jax.ShapeDtypeStruct((1, SB), F32)),
            in_specs=[hbm, hbm, vmem, vmem],
            out_specs=(vmem, vmem),
            scratch_shapes=[
                pltpu.VMEM((n_sum, k_rows, cols), BF16),
                pltpu.VMEM((n_steps * batch, cols), BF16),
                pltpu.VMEM((n_blocks, n_sum, block_rows, cols), BF16),
                pltpu.VMEM((2, block_rows, k_rows), F32),
                pltpu.VMEM((2, n_gather, 2, batch, SB), F32),
                pltpu.VMEM((2, n_gather, 1, SB), F32),
                pltpu.VMEM((2, n_sum, 1, SB), F32),
                pltpu.VMEM((2, n_sum - 1, 2, batch, SB), F32),
                pltpu.VMEM((n_sum - 1, 2, batch, SB), F32),
                pltpu.VMEM((batch, k_rows), BF16),
                pltpu.VMEM((batch, SB), F32),
                pltpu.VMEM((2, batch, SB), F32),
                pltpu.VMEM((1, SB), F32),
                pltpu.VMEM((batch, SB), F32),
                pltpu.VMEM((1, SB), F32),
                pltpu.SemaphoreType.REGULAR,
                dma((n_sum, 2)), dma((n_sum,)), dma, dma, dma((2, n_sum)), dma, dma, dma((2,)),
                dma((2,)), dma, dma((2,)), dma, dma((2,)), dma, dma((2,)), dma, dma((2,)), dma((2,)),
            ],
            compiler_params=pltpu.CompilerParams(collective_id=0, has_side_effects=True,
                                                 vmem_limit_bytes=48 * 1024 * 1024),
            cost_estimate=pl.CostEstimate(flops=2 * batch * (n_steps - 1) * n_sum * k_rows * cols,
                                          bytes_accessed=n_sum * k_rows * cols * 2, transcendentals=0),
        )(a_blk, emis.reshape(n_steps * batch, SB), first_raw, len_row)
        return ll[0, :batch], alpha

    return jax.shard_map(local_forward, mesh=mesh, in_specs=(P('rows', None, 'states'), P(vec_axes, None), P(vec_axes), P('seqs', None), P('seqs')), out_specs=(P('seqs'), P('seqs', vec_axes)), check_vma=False)
```

time: 1060 us -> 983 us (0.927)
  Pallas kernels: 1050 us -> 970 us
    pallas_call x1, Pallas kernels: 1050 us -> 970 us  [local_forward(): pl.pallas_call(functools.partial(forward_kernel, CHIPS, n_steps, block),...]
where the time goes in v6:
time: 983 us
  Pallas kernels  970 us (99%)
  local copies, waits for them, and re-layouts  11.9 us (1%)
    pallas_call x1, Pallas kernels, local_forward(): pl.pallas_call(functools.partial(forward_kernel, CHIPS, n_steps, block),...  970 us

profile of v6, /device:TPU:1, one launch (start us, length us, event | category | flops | bytes accessed | tf_op | source)
XLA Modules:
  0.0 983.0 jit_solution(16394720470096397990)
XLA Ops:
  0.6 0.0 copy-start
  0.6 0.0 copy-start.1
  0.7 0.8 convert_element_type.13
  1.5 0.7 slice_bitcast_fusion
  2.2 0.8 slice_bitcast_fusion.1
  2.9 0.1 fusion.1
  3.0 0.0 copy-done
  3.0 6.2 gather_fusion
  9.3 0.3 copy.15
  9.6 0.0 copy-done.1
  9.6 2.7 copy.14
  12.4 969.5 %shard_map.68 = (f32[16,128]{1,0:T(8,128)S(1)}, f32[1,128]{1,0:T(1,128)S(1)}) custom-call(bf16[8192,256]{1,0:T(8,128)(2,1)S(1)} %bitcast.27, bf16[2048,128]{1,0:T(8,128)(2,1)S(1)} %bitcast.29, f32[16,128]{1,0:T(8,128)S(1)} %convert_multiply_fusion.r0_ref, f32[1,128]{1,0:T(1,128)S(1)} %pad_bitcast_fusion.len_ref), custom_call_target="tpu_custom_call" | custom-call | flops 17045651456 | bytes 8388608 | tf_op jit(solution)/shard_map/pallas_call | solution.py:310
  981.9 0.5 slice_bitcast_fusion.3
  982.4 0.6 copy.17
  (3 shorter events, 0.1 us)
Async XLA Ops:
  0.6 2.4 copy-start
  0.6 9.0 copy-start.1

commit v7 on v6

--- a/solution.py
+++ b/solution.py
@@ -10,8 +10,9 @@
 CHIPS = (4, 4, 4)
 SB = 128
 LIFT = 2.0 ** 64
-LAG = 1
-P_AFTER = 1
+LAG = 2
+P_AFTER = 2
+NEAR = 4
 BLOCK = 8
 AHEAD = 6
 F32 = jnp.float32
@@ -23,7 +24,7 @@
 
 
 def forward_kernel(dims, n_steps, block, a_ref, e_ref, r0_ref, len_ref, alpha_ref, ll_ref,
-                   a_loc, e_both, e_loc, w_loc, r_in, c_in, p_in, u_in, u_out, a_bf, len_col, alpha_acc, ll_acc,
+                   a_loc, e_both, e_loc, w_loc, r_in, c_in, p_in, u_in, u_out, a_bf, len_row, len_col, alpha_acc, ll_acc,
                    fin_alpha, fin_ll, tick, a_sem, a_send, e_pair, e_send, e_sem, r0_sem, r0_send, own_sem,
                    g_recv, g_send, c_recv, c_send, u_recv, u_send, p_recv, p_send, f_recv, f_send):
     nz, ny, nx = dims
@@ -39,11 +40,13 @@
     y = (me // nx) % ny
     x = me % nx
     group = me // n_gather
-    place = me % n_gather
     c_place = (((y + 1) // 2) % 2) * nx + x
     far = sorted(range(1, n_sum), key=lambda k: -(ring_distance(k // 2, nz) + k % 2))
-    far_gather = sorted(((f, d) for f in range(2) for d in range(nx) if f or d),
-                        key=lambda o: -(o[0] + ring_distance(o[1], nx)))
+    sources = sorted(((f, d) for f in range(2) for d in range(nx)), key=lambda o: o[0] + ring_distance(o[1], nx))
+    slot_of = {o: i for i, o in enumerate(sources)}
+    far_gather = sources[:0:-1]
+    n_near = n_gather // 2
+    n_far = n_gather - n_near
 
     def sum_peer(k, sign=1):
         flip = k % 2
@@ -63,13 +66,18 @@
     def wait_bytes(ref, sem):
         pltpu.make_async_copy(ref, ref, sem).wait()
 
-    def a_copy(h, k):
+    def a_rows(state, h):
+        for i, (f, d) in enumerate(sources):
+            there = ((state // nx + f) % 2) * nx + (x + d) % nx
+            yield (a_ref.at[pl.ds((state // n_gather) * half + there * SB, SB)], pl.ds((2 * i + h) * SB, SB))
+
+    def start_a(h, k):
         peer = sum_peer(k, -1)
-        return remote(a_ref.at[pl.ds((peer // n_gather) * half, half)], a_loc.at[k, pl.ds(h * half, half)],
-                      a_send.at[k], a_sem.at[k, h], peer)
+        for src, to in a_rows(peer, h):
+            remote(src, a_loc.at[k, to], a_send.at[k], a_sem.at[k, h], peer).start()
 
     def e_copy(b, k):
-        return remote(e_both.at[pl.ds(b * rows, rows)], e_loc.at[b, k], e_send, e_sem.at[b % 2, k], sum_peer(k, -1))
+        return remote(e_both.at[pl.ds(b * rows + batch, rows)], e_loc.at[b, k], e_send, e_sem.at[b % 2, k], sum_peer(k, -1))
 
     barrier = pltpu.get_barrier_semaphore()
 
@@ -80,19 +88,20 @@
     def helper():
         announce(me, 1)
         pl.semaphore_wait(barrier, n_sum)
-        first = remote(r0_ref, r_in.at[0, place, 0], r0_send, r0_sem, me)
+        first = remote(r0_ref, r_in.at[0, 0, 0], r0_send, r0_sem, me)
         first.start()
-        mine = pltpu.make_async_copy(e_ref, e_both.at[:, pl.ds(0, SB)], own_sem.at[0])
+        every = pl.ds(0, n_steps * batch)
+        mine = pltpu.make_async_copy(e_ref, e_both.at[every, pl.ds(0, SB)], own_sem.at[0])
         mine.start()
-        copies = [a_copy(0, k) for k in range(n_sum)]
-        copies[0].start()
-        copies[1].start()
+        e_both[pl.ds(n_steps * batch, batch), :] = jnp.zeros((batch, 2 * SB), BF16)
+        start_a(0, 0)
+        start_a(0, 1)
         mine.wait()
-        wait_bytes(e_both.at[:, pl.ds(SB, SB)], e_pair)
+        wait_bytes(e_both.at[every, pl.ds(SB, SB)], e_pair)
         e_copy(0, 0).start()
         e_copy(0, 1).start()
         for k in range(2, n_sum):
-            copies[k].start()
+            start_a(0, k)
             e_copy(0, k).start()
         wait_bytes(e_loc.at[0], e_send)
 
@@ -108,8 +117,8 @@
 
         lax.fori_loop(0, n_steps - block, send_part, 0)
         first.wait_send()
-        for copy in copies:
-            copy.wait_send()
+        for k in range(n_sum):
+            wait_bytes(a_loc.at[k, pl.ds(0, half)], a_send.at[k])
         wait_bytes(fin_alpha, f_recv.at[0])
         wait_bytes(fin_ll, f_recv.at[1])
         alpha_ref[...] = fin_alpha[...]
@@ -128,8 +137,10 @@
             return jnp.sum(jnp.where(eye, row, 0.0), axis=1, keepdims=True)
 
         def start_gather(slot):
-            for o in far_gather:
-                remote(r_in.at[slot, place], r_in.at[slot, place], g_send, g_recv.at[slot], gather_peer(*o)).start()
+            for f, d in far_gather:
+                there = slot_of[f, (nx - d) % nx]
+                remote(r_in.at[slot, 0], r_in.at[slot, there], g_send, g_recv.at[slot, there // n_near],
+                       gather_peer(f, d)).start()
 
         def start_parts(slot):
             for k in far:
@@ -143,6 +154,13 @@
             c_in[slot, c_place] = jnp.sum(p_in[slot], axis=0)
             for o in far_gather:
                 remote(c_in.at[slot, c_place], c_in.at[slot, c_place], c_send, c_recv.at[slot], gather_peer(*o)).start()
+
+        def wait_near(slot):
+            if n_near > 1:
+                wait_bytes(r_in.at[slot, pl.ds(0, n_near - 1)], g_recv.at[slot, 0])
+
+        def wait_far(slot):
+            wait_bytes(r_in.at[slot, pl.ds(0, n_far)], g_recv.at[slot, 1])
 
         def norm(slot):
             wait_bytes(c_in.at[slot, others], c_recv.at[slot])
@@ -155,8 +173,8 @@
             now = lax.convert_element_type(t, F32)
             active = now < len_col[...]
             for h in range(2):
-                alpha_acc[h] = jnp.where(active, r_in[slot, place, h] * inv, alpha_acc[h])
-            ll_acc[...] = ll_acc[...] + jnp.where(now < len_ref[...], jnp.log(c_row * (1.0 / LIFT)), 0.0)
+                alpha_acc[h] = jnp.where(active, r_in[slot, 0, h] * inv, alpha_acc[h])
+            ll_acc[...] = ll_acc[...] + jnp.where(now < len_row[...], jnp.log(c_row * (1.0 / LIFT)), 0.0)
 
         def add_w(b, k, fresh):
             part = lax.dot_general(e_loc[b, k], a_loc[k], (((1,), (1,)), ((), ())), preferred_element_type=F32)
@@ -170,32 +188,33 @@
         for k in range(n_sum):
             announce(sum_peer(k), 0)
         pl.semaphore_wait(barrier, n_sum + n_gather - 1)
-        pair = remote(e_ref, e_both.at[:, pl.ds(SB, SB)], own_sem.at[0], e_pair, me, to=0)
+        pair = remote(e_ref, e_both.at[pl.ds(0, n_steps * batch), pl.ds(SB, SB)], own_sem.at[0], e_pair, me, to=0)
         pair.start()
-        copies = [a_copy(1, k) for k in range(1, n_sum)]
-        for copy in copies:
-            copy.start()
-        own = pltpu.make_async_copy(a_ref.at[pl.ds(group * half, half)], a_loc.at[0, pl.ds(half, half)], own_sem.at[1])
-        own.start()
+        for k in range(1, n_sum):
+            start_a(1, k)
+        for src, to in a_rows(me, 1):
+            pltpu.make_async_copy(src, a_loc.at[0, to], own_sem.at[1]).start()
         alpha_acc[...] = jnp.zeros_like(alpha_acc)
         ll_acc[...] = jnp.zeros_like(ll_acc)
         w_loc[...] = jnp.zeros_like(w_loc)
-        len_col[...] = jnp.broadcast_to(as_col(len_ref[...]), (batch, SB))
-        r_in[0, place, 1] = r0_ref[...]
+        len_row[...] = jnp.zeros_like(len_row)
+        len_row[:, :batch] = len_ref[...].astype(F32)
+        len_col[...] = jnp.broadcast_to(as_col(len_row[...]), (batch, SB))
+        r_in[0, 0, 1] = r0_ref[...]
         wait_bytes(r0_ref, r0_sem)
-        p_in[0, group] = as_row(r_in[0, place, 0] + r_in[0, place, 1])
+        p_in[0, group] = as_row(r_in[0, 0, 0] + r_in[0, 0, 1])
         start_parts(0)
         start_gather(0)
         finish_norm(0)
         wait_bytes(p_in.at[0, peers], p_send)
-        own.wait()
+        wait_bytes(a_loc.at[0, pl.ds(0, half)], own_sem.at[1])
 
         def first_w(k, carry):
             wait_bytes(a_loc.at[k, pl.ds(0, half)], a_sem.at[k, 0])
 
             @pl.when(k > 0)
             def from_owner():
-                wait_bytes(a_loc.at[k, pl.ds(half, half)], a_sem.at[k, 1])
+                wait_bytes(a_loc.at[k, pl.ds(0, half)], a_sem.at[k, 1])
 
             wait_bytes(e_loc.at[0, k], e_sem.at[0, k])
             add_w(0, k, False)
@@ -203,8 +222,8 @@
 
         lax.fori_loop(0, n_sum, first_w, 0)
         pair.wait_send()
-        for copy in copies:
-            copy.wait_send()
+        for k in range(1, n_sum):
+            wait_bytes(a_loc.at[k, pl.ds(0, half)], a_send.at[k])
 
         def one_step(t, carry):
             cur = t % 2
@@ -212,14 +231,27 @@
             b = t // block
             row = pl.ds((t % block) * batch, batch)
             c_row, inv = norm(cur)
-            wait_bytes(r_in.at[cur, others], g_recv.at[cur])
             total = jnp.zeros((batch, SB), F32)
-            for h in range(2):
-                for src in range(n_gather):
-                    cols = pl.ds(h * half + src * SB, SB)
-                    tile = (r_in[cur, src, h] * inv).astype(BF16)
-                    a_bf[:, cols] = tile
-                    total = total + tile.astype(F32) * w_loc[b % 2, row, cols]
+
+            def take(first, last, total):
+                for i in range(first, last):
+                    for h in range(2):
+                        cols = pl.ds((2 * i + h) * SB, SB)
+                        tile = (r_in[cur, i, h] * inv).astype(BF16)
+                        a_bf[:, cols] = tile
+                        total = total + tile.astype(F32) * w_loc[b % 2, row, cols]
+                return total
+
+            def times(k, first, last):
+                return jnp.dot(a_bf[:, first:last], a_loc[k, first:last], preferred_element_type=F32)
+
+            order = far + [0]
+            near_rows, all_rows = 2 * n_near * SB, 2 * half
+            wait_near(cur)
+            total = take(0, n_near, total)
+            near = [times(k, 0, near_rows) for k in order[:NEAR]]
+            wait_far(cur)
+            total = take(n_near, n_gather, total)
             unit = jnp.where(t >= 0, jnp.float32(1.0), jnp.float32(0.0))
             ready = []
 
@@ -229,10 +261,11 @@
                     u_out[k - 1, h] = part[:, h * SB:(h + 1) * SB]
                 remote(u_out.at[k - 1], u_in.at[nxt, mirror(k) - 1], u_send, u_recv.at[nxt], sum_peer(k)).start()
 
-            for i, k in enumerate(far + [0]):
-                low = jnp.dot(a_bf[:, :half], a_loc[k, :half], preferred_element_type=F32)
-                high = jnp.dot(a_bf[:, half:], a_loc[k, half:], preferred_element_type=F32)
-                ready.append((k, low * unit + high))
+            for i, k in enumerate(order):
+                begin = near_rows if i < NEAR else 0
+                middle = (begin + all_rows) // 2
+                part = times(k, begin, middle) * unit + times(k, middle, all_rows)
+                ready.append((k, part + near[i] if i < NEAR else part))
                 if i == P_AFTER:
                     p_in[nxt, group] = as_row(total)
                     start_parts(nxt)
@@ -250,7 +283,7 @@
                 parts = [own_part[:, h * SB:(h + 1) * SB]] + [u_in[nxt, k, h] for k in range(n_sum - 1)]
                 while len(parts) > 1:
                     parts = [parts[i] + parts[i + 1] for i in range(0, len(parts), 2)]
-                r_in[nxt, place, h] = parts[0] * e_loc[b, 0, row, pl.ds(h * SB, SB)].astype(F32)
+                r_in[nxt, 0, h] = parts[0] * e_loc[b, 0, row, pl.ds(h * SB, SB)].astype(F32)
             start_gather(nxt)
 
             @pl.when(t < n_steps - block - AHEAD)
@@ -273,7 +306,8 @@
         lax.fori_loop(0, n_steps - 1, one_step, 0)
         last = (n_steps - 1) % 2
         c_row, inv = norm(last)
-        wait_bytes(r_in.at[last, others], g_recv.at[last])
+        wait_near(last)
+        wait_far(last)
         keep(n_steps - 1, last, c_row, inv)
         wait_bytes(r_in.at[last, others], g_send)
         wait_bytes(c_in.at[last, others], c_send)
@@ -296,10 +330,9 @@
         batch, n_steps = tokens.shape
         cols = 2 * SB
         a_blk = trans_blk.reshape(trans_blk.shape[0], cols)
-        emis = jnp.transpose(emit_blk.at[:, jnp.roll(tokens, -1, axis=1)].get(mode='promise_in_bounds'), (2, 1, 0))
+        emis = jnp.transpose(emit_blk.at[:, tokens].get(mode='promise_in_bounds'), (2, 1, 0))
         emis = emis * jnp.asarray(LIFT, emis.dtype)
-        first_raw = init_blk[None, :] * emis[-1].astype(F32)
-        len_row = jnp.pad(lengths.astype(F32), (0, SB - batch))[None, :]
+        first_raw = init_blk[None, :] * emis[0].astype(F32)
         vmem = pl.BlockSpec(memory_space=pltpu.VMEM)
         hbm = pl.BlockSpec(memory_space=pl.ANY)
         dma = pltpu.SemaphoreType.DMA
@@ -314,7 +347,7 @@
             out_specs=(vmem, vmem),
             scratch_shapes=[
                 pltpu.VMEM((n_sum, k_rows, cols), BF16),
-                pltpu.VMEM((n_steps * batch, cols), BF16),
+                pltpu.VMEM(((n_steps + 1) * batch, cols), BF16),
                 pltpu.VMEM((n_blocks, n_sum, block_rows, cols), BF16),
                 pltpu.VMEM((2, block_rows, k_rows), F32),
                 pltpu.VMEM((2, n_gather, 2, batch, SB), F32),
@@ -323,6 +356,7 @@
                 pltpu.VMEM((2, n_sum - 1, 2, batch, SB), F32),
                 pltpu.VMEM((n_sum - 1, 2, batch, SB), F32),
                 pltpu.VMEM((batch, k_rows), BF16),
+                pltpu.VMEM((1, SB), F32),
                 pltpu.VMEM((batch, SB), F32),
                 pltpu.VMEM((2, batch, SB), F32),
                 pltpu.VMEM((1, SB), F32),
@@ -330,13 +364,13 @@
                 pltpu.VMEM((1, SB), F32),
                 pltpu.SemaphoreType.REGULAR,
                 dma((n_sum, 2)), dma((n_sum,)), dma, dma, dma((2, n_sum)), dma, dma, dma((2,)),
-                dma((2,)), dma, dma((2,)), dma, dma((2,)), dma, dma((2,)), dma, dma((2,)), dma((2,)),
+                dma((2, 2)), dma, dma((2,)), dma, dma((2,)), dma, dma((2,)), dma, dma((2,)), dma((2,)),
             ],
             compiler_params=pltpu.CompilerParams(collective_id=0, has_side_effects=True,
                                                  vmem_limit_bytes=48 * 1024 * 1024),
             cost_estimate=pl.CostEstimate(flops=2 * batch * (n_steps - 1) * n_sum * k_rows * cols,
                                           bytes_accessed=n_sum * k_rows * cols * 2, transcendentals=0),
-        )(a_blk, emis.reshape(n_steps * batch, SB), first_raw, len_row)
+        )(a_blk, emis.reshape(n_steps * batch, SB), first_raw, lengths[None, :])
         return ll[0, :batch], alpha
 
     return jax.shard_map(local_forward, mesh=mesh, in_specs=(P('rows', None, 'states'), P(vec_axes, None), P(vec_axes), P('seqs', None), P('seqs')), out_specs=(P('seqs'), P('seqs', vec_axes)), check_vma=False)

time: 983 us -> 995 us (1.012)
  Pallas kernels: 970 us -> 982 us
    pallas_call x1, Pallas kernels: 970 us -> 982 us  [local_forward(): pl.pallas_call(functools.partial(forward_kernel, CHIPS, n_steps, block),...]
where the time goes in v7:
time: 995 us
  Pallas kernels  982 us (99%)
  local copies, waits for them, and re-layouts  11.3 us (1%)
    pallas_call x1, Pallas kernels, local_forward(): pl.pallas_call(functools.partial(forward_kernel, CHIPS, n_steps, block),...  982 us

profile of v7, /device:TPU:1, one launch (start us, length us, event | category | flops | bytes accessed | tf_op | source)
XLA Modules:
  0.0 995.1 jit_solution(13031763985802826315)
XLA Ops:
  0.6 0.0 copy-start
  0.6 0.0 copy-start.2
  0.7 0.9 fusion.1
  1.5 0.9 copy-done
  2.4 6.2 gather_fusion
  8.6 0.3 copy.13
  9.0 0.0 copy-done.2
  9.0 0.0 copy-start.1
  9.0 2.7 copy.12
  11.7 0.0 copy-done.1
  11.7 982.3 %shard_map.68 = (f32[16,128]{1,0:T(8,128)S(1)}, f32[1,128]{1,0:T(1,128)S(1)}) custom-call(bf16[8192,256]{1,0:T(8,128)(2,1)S(1)} %bitcast.22, bf16[2048,128]{1,0:T(8,128)(2,1)S(1)} %bitcast.24, f32[16,128]{1,0:T(8,128)S(1)} %convert_multiply_fusion.r0_ref, s32[1,16]{1,0:T(1,128)S(1)} %bitcast.25), custom_call_target="tpu_custom_call" | custom-call | flops 17045651456 | bytes 8388608 | tf_op jit(solution)/shard_map/pallas_call | solution.py:343
  994.0 0.5 slice_bitcast_fusion.1
  994.5 0.6 copy.15
  (2 shorter events, 0.1 us)
Async XLA Ops:
  0.6 1.7 copy-start
  0.6 8.3 copy-start.2
  9.0 2.8 copy-start.1

commit v8 on v7

--- a/solution.py
+++ b/solution.py
@@ -10,9 +10,9 @@
 CHIPS = (4, 4, 4)
 SB = 128
 LIFT = 2.0 ** 64
-LAG = 2
-P_AFTER = 2
-NEAR = 4
+LAG = 1
+P_AFTER = 1
+NEAR = 2
 BLOCK = 8
 AHEAD = 6
 F32 = jnp.float32

time: 995 us -> 988 us (level)
  no operation moved by 1% of the time
where the time goes in v8:
time: 988 us
  Pallas kernels  975 us (99%)
  local copies, waits for them, and re-layouts  11.3 us (1%)
    pallas_call x1, Pallas kernels, local_forward(): pl.pallas_call(functools.partial(forward_kernel, CHIPS, n_steps, block),...  975 us

profile of v8, /device:TPU:1, one launch (start us, length us, event | category | flops | bytes accessed | tf_op | source)
XLA Modules:
  0.0 988.1 jit_solution(16593906273370890112)
XLA Ops:
  0.6 0.0 copy-start
  0.6 0.0 copy-start.2
  0.7 0.9 fusion.1
  1.5 0.9 copy-done
  2.4 6.2 gather_fusion
  8.6 0.3 copy.13
  9.0 0.0 copy-done.2
  9.0 0.0 copy-start.1
  9.0 2.7 copy.12
  11.7 0.0 copy-done.1
  11.8 975.2 %shard_map.68 = (f32[16,128]{1,0:T(8,128)S(1)}, f32[1,128]{1,0:T(1,128)S(1)}) custom-call(bf16[8192,256]{1,0:T(8,128)(2,1)S(1)} %bitcast.22, bf16[2048,128]{1,0:T(8,128)(2,1)S(1)} %bitcast.24, f32[16,128]{1,0:T(8,128)S(1)} %convert_multiply_fusion.r0_ref, s32[1,16]{1,0:T(1,128)S(1)} %bitcast.25), custom_call_target="tpu_custom_call" | custom-call | flops 17045651456 | bytes 8388608 | tf_op jit(solution)/shard_map/pallas_call | solution.py:343
  987.0 0.5 slice_bitcast_fusion.1
  987.5 0.6 copy.15
  (2 shorter events, 0.1 us)
Async XLA Ops:
  0.6 1.7 copy-start
  0.6 8.3 copy-start.2
  9.0 2.8 copy-start.1

commit v9 on v8

--- a/solution.py
+++ b/solution.py
@@ -12,7 +12,7 @@
 LIFT = 2.0 ** 64
 LAG = 1
 P_AFTER = 1
-NEAR = 2
+NEAR = 0
 BLOCK = 8
 AHEAD = 6
 F32 = jnp.float32

time: 988 us -> 976 us (0.988)
  Pallas kernels: 975 us -> 963 us
    pallas_call x1, Pallas kernels: 975 us -> 963 us  [local_forward(): pl.pallas_call(functools.partial(forward_kernel, CHIPS, n_steps, block),...]
where the time goes in v9:
time: 976 us
  Pallas kernels  963 us (99%)
  local copies, waits for them, and re-layouts  11.3 us (1%)
    pallas_call x1, Pallas kernels, local_forward(): pl.pallas_call(functools.partial(forward_kernel, CHIPS, n_steps, block),...  963 us

profile of v9, /device:TPU:1, one launch (start us, length us, event | category | flops | bytes accessed | tf_op | source)
XLA Modules:
  0.0 975.8 jit_solution(4938282243239020977)
XLA Ops:
  0.6 0.0 copy-start
  0.6 0.0 copy-start.2
  0.7 0.9 fusion.1
  1.5 0.9 copy-done
  2.4 6.2 gather_fusion
  8.6 0.3 copy.13
  9.0 0.0 copy-done.2
  9.0 0.0 copy-start.1
  9.0 2.7 copy.12
  11.7 0.0 copy-done.1
  11.7 962.9 %shard_map.68 = (f32[16,128]{1,0:T(8,128)S(1)}, f32[1,128]{1,0:T(1,128)S(1)}) custom-call(bf16[8192,256]{1,0:T(8,128)(2,1)S(1)} %bitcast.22, bf16[2048,128]{1,0:T(8,128)(2,1)S(1)} %bitcast.24, f32[16,128]{1,0:T(8,128)S(1)} %convert_multiply_fusion.r0_ref, s32[1,16]{1,0:T(1,128)S(1)} %bitcast.25), custom_call_target="tpu_custom_call" | custom-call | flops 17045651456 | bytes 8388608 | tf_op jit(solution)/shard_map/pallas_call | solution.py:343
  974.7 0.5 slice_bitcast_fusion.1
  975.2 0.6 copy.15
  (2 shorter events, 0.1 us)
Async XLA Ops:
  0.6 1.7 copy-start
  0.6 8.3 copy-start.2
  9.0 2.8 copy-start.1

commit v10 on v9

--- a/solution.py
+++ b/solution.py
@@ -23,13 +23,13 @@
     return min(offset, n - offset)
 
 
-def forward_kernel(dims, n_steps, block, a_ref, e_ref, r0_ref, len_ref, alpha_ref, ll_ref,
+def forward_kernel(dims, n_steps, block, a_ref, emit_ref, init_ref, tok_ref, len_ref, alpha_ref, ll_ref,
                    a_loc, e_both, e_loc, w_loc, r_in, c_in, p_in, u_in, u_out, a_bf, len_row, len_col, alpha_acc, ll_acc,
-                   fin_alpha, fin_ll, tick, a_sem, a_send, e_pair, e_send, e_sem, r0_sem, r0_send, own_sem,
+                   fin_alpha, fin_ll, by_word, picked, e_half, r0_own, tick, a_sem, a_send, e_pair, e_send, e_sem, r0_sem, r0_send, own_sem,
                    g_recv, g_send, c_recv, c_send, u_recv, u_send, p_recv, p_send, f_recv, f_send):
     nz, ny, nx = dims
     n_sum, n_gather = 2 * nz, 2 * nx
-    batch = r0_ref.shape[0]
+    batch = tok_ref.shape[0]
     half = n_gather * SB
     rows = block * batch
     n_blocks = n_steps // block
@@ -79,6 +79,30 @@
     def e_copy(b, k):
         return remote(e_both.at[pl.ds(b * rows + batch, rows)], e_loc.at[b, k], e_send, e_sem.at[b % 2, k], sum_peer(k, -1))
 
+    def pick_tokens():
+        n_words = emit_ref.shape[1]
+
+        def turn(first, count):
+            tile = emit_ref[:, pl.ds(first, count)].astype(F32) * LIFT
+            by_word[pl.ds(first, count), :] = tile.T
+
+        def turn_tiles(i, carry):
+            turn(pl.multiple_of(i * SB, SB), SB)
+            return carry
+
+        lax.fori_loop(0, n_words // SB, turn_tiles, 0, unroll=2)
+        if n_words % SB:
+            turn(n_words // SB * SB, n_words % SB)
+
+        def pick(t, carry):
+            for b in range(batch):
+                picked[t, b:b + 1, :] = by_word[pl.ds(tok_ref[b, t], 1), :]
+            e_half[pl.ds(pl.multiple_of(t * batch, batch), batch), :] = picked[t].astype(BF16)
+            return carry
+
+        lax.fori_loop(0, n_steps, pick, 0)
+        r0_own[...] = picked[0] * init_ref[...]
+
     barrier = pltpu.get_barrier_semaphore()
 
     def announce(state, to):
@@ -88,20 +112,18 @@
     def helper():
         announce(me, 1)
         pl.semaphore_wait(barrier, n_sum)
-        first = remote(r0_ref, r_in.at[0, 0, 0], r0_send, r0_sem, me)
+        for k in range(n_sum):
+            start_a(0, k)
+        e_both[pl.ds(n_steps * batch, batch), :] = jnp.zeros((batch, 2 * SB), BF16)
+        pick_tokens()
+        first = remote(r0_own, r_in.at[0, 0, 0], r0_send, r0_sem, me)
         first.start()
         every = pl.ds(0, n_steps * batch)
-        mine = pltpu.make_async_copy(e_ref, e_both.at[every, pl.ds(0, SB)], own_sem.at[0])
+        mine = pltpu.make_async_copy(e_half, e_both.at[every, pl.ds(0, SB)], own_sem.at[0])
         mine.start()
-        e_both[pl.ds(n_steps * batch, batch), :] = jnp.zeros((batch, 2 * SB), BF16)
-        start_a(0, 0)
-        start_a(0, 1)
         mine.wait()
         wait_bytes(e_both.at[every, pl.ds(SB, SB)], e_pair)
-        e_copy(0, 0).start()
-        e_copy(0, 1).start()
-        for k in range(2, n_sum):
-            start_a(0, k)
+        for k in range(n_sum):
             e_copy(0, k).start()
         wait_bytes(e_loc.at[0], e_send)
 
@@ -122,7 +144,7 @@
         wait_bytes(fin_alpha, f_recv.at[0])
         wait_bytes(fin_ll, f_recv.at[1])
         alpha_ref[...] = fin_alpha[...]
-        ll_ref[...] = fin_ll[...]
+        ll_ref[...] = fin_ll[:, :batch]
 
     @pl.when(core == 1)
     def owner():
@@ -188,20 +210,21 @@
         for k in range(n_sum):
             announce(sum_peer(k), 0)
         pl.semaphore_wait(barrier, n_sum + n_gather - 1)
-        pair = remote(e_ref, e_both.at[pl.ds(0, n_steps * batch), pl.ds(SB, SB)], own_sem.at[0], e_pair, me, to=0)
-        pair.start()
         for k in range(1, n_sum):
             start_a(1, k)
         for src, to in a_rows(me, 1):
             pltpu.make_async_copy(src, a_loc.at[0, to], own_sem.at[1]).start()
+        pick_tokens()
         alpha_acc[...] = jnp.zeros_like(alpha_acc)
         ll_acc[...] = jnp.zeros_like(ll_acc)
         w_loc[...] = jnp.zeros_like(w_loc)
         len_row[...] = jnp.zeros_like(len_row)
         len_row[:, :batch] = len_ref[...].astype(F32)
         len_col[...] = jnp.broadcast_to(as_col(len_row[...]), (batch, SB))
-        r_in[0, 0, 1] = r0_ref[...]
-        wait_bytes(r0_ref, r0_sem)
+        pair = remote(e_half, e_both.at[pl.ds(0, n_steps * batch), pl.ds(SB, SB)], own_sem.at[0], e_pair, me, to=0)
+        pair.start()
+        r_in[0, 0, 1] = r0_own[...]
+        wait_bytes(r0_own, r0_sem)
         p_in[0, group] = as_row(r_in[0, 0, 0] + r_in[0, 0, 1])
         start_parts(0)
         start_gather(0)
@@ -316,7 +339,7 @@
         for copy in result:
             copy.start()
         alpha_ref[...] = alpha_acc[1]
-        ll_ref[...] = ll_acc[...]
+        ll_ref[...] = ll_acc[:, :batch]
         for copy in result:
             copy.wait_send()
 
@@ -330,9 +353,6 @@
         batch, n_steps = tokens.shape
         cols = 2 * SB
         a_blk = trans_blk.reshape(trans_blk.shape[0], cols)
-        emis = jnp.transpose(emit_blk.at[:, tokens].get(mode='promise_in_bounds'), (2, 1, 0))
-        emis = emis * jnp.asarray(LIFT, emis.dtype)
-        first_raw = init_blk[None, :] * emis[0].astype(F32)
         vmem = pl.BlockSpec(memory_space=pltpu.VMEM)
         hbm = pl.BlockSpec(memory_space=pl.ANY)
         dma = pltpu.SemaphoreType.DMA
@@ -342,8 +362,8 @@
         n_blocks = n_steps // block
         alpha, ll = pl.pallas_call(
             functools.partial(forward_kernel, CHIPS, n_steps, block),
-            out_shape=(jax.ShapeDtypeStruct((batch, SB), F32), jax.ShapeDtypeStruct((1, SB), F32)),
-            in_specs=[hbm, hbm, vmem, vmem],
+            out_shape=(jax.ShapeDtypeStruct((batch, SB), F32), jax.ShapeDtypeStruct((1, batch), F32)),
+            in_specs=[hbm, vmem, vmem, pl.BlockSpec(memory_space=pltpu.SMEM), vmem],
             out_specs=(vmem, vmem),
             scratch_shapes=[
                 pltpu.VMEM((n_sum, k_rows, cols), BF16),
@@ -362,6 +382,10 @@
                 pltpu.VMEM((1, SB), F32),
                 pltpu.VMEM((batch, SB), F32),
                 pltpu.VMEM((1, SB), F32),
+                pltpu.VMEM((emit_blk.shape[1], SB), F32),
+                pltpu.VMEM((n_steps, batch, SB), F32),
+                pltpu.VMEM((n_steps * batch, SB), BF16),
+                pltpu.VMEM((batch, SB), F32),
                 pltpu.SemaphoreType.REGULAR,
                 dma((n_sum, 2)), dma((n_sum,)), dma, dma, dma((2, n_sum)), dma, dma, dma((2,)),
                 dma((2, 2)), dma, dma((2,)), dma, dma((2,)), dma, dma((2,)), dma, dma((2,)), dma((2,)),
@@ -370,7 +394,7 @@
                                                  vmem_limit_bytes=48 * 1024 * 1024),
             cost_estimate=pl.CostEstimate(flops=2 * batch * (n_steps - 1) * n_sum * k_rows * cols,
                                           bytes_accessed=n_sum * k_rows * cols * 2, transcendentals=0),
-        )(a_blk, emis.reshape(n_steps * batch, SB), first_raw, lengths[None, :])
-        return ll[0, :batch], alpha
+        )(a_blk, emit_blk, init_blk[None, :], tokens, lengths[None, :])
+        return ll[0], alpha
 
     return jax.shard_map(local_forward, mesh=mesh, in_specs=(P('rows', None, 'states'), P(vec_axes, None), P(vec_axes), P('seqs', None), P('seqs')), out_specs=(P('seqs'), P('seqs', vec_axes)), check_vma=False)

time: 976 us -> 974 us (level)
  no operation moved by 1% of the time
where the time goes in v10:
time: 974 us
  Pallas kernels  964 us (99%)
    pallas_call x1, Pallas kernels, local_forward(): pl.pallas_call(functools.partial(forward_kernel, CHIPS, n_steps, block),...  964 us

profile of v10, /device:TPU:1, one launch (start us, length us, event | category | flops | bytes accessed | tf_op | source)
XLA Modules:
  0.0 974.1 jit_solution(9448116927284559256)
XLA Ops:
  0.6 3.2 copy.7.emit_ref
  3.8 0.0 copy-start
  3.8 0.0 copy-start.1
  3.8 0.0 copy-start.2
  3.8 4.7 copy.10
  8.5 0.0 copy-done
  8.5 0.0 copy-done.1
  8.5 0.0 copy-done.2
  8.5 964.5 %shard_map.68 = (f32[16,128]{1,0:T(8,128)S(1)}, f32[1,16]{1,0:T(1,128)S(1)}) custom-call(bf16[8192,256]{1,0:T(8,128)(2,1)} %bitcast.11, bf16[128,10000]{1,0:T(8,128)(2,1)S(1)} %copy.7.emit_ref, f32[1,128]{1,0:T(1,128)S(1)} %bitcast.7, s32[16,128]{1,0:T(8,128)S(1)} %copy-done, s32[1,16]{1,0:T(1,128)S(1)} %bitcast.8), custom_call_target="tpu_custom_call" | custom-call | flops 17045651456 | bytes 8388608 | tf_op jit(solution)/shard_map/pallas_call | solution.py:363
  973.0 0.5 copy.13
  973.5 0.6 copy.14
Async XLA Ops:
  3.8 4.7 copy-start
  3.8 4.7 copy-start.1
  3.8 4.7 copy-start.2

commit v11 on v10

--- a/solution.py
+++ b/solution.py
@@ -80,19 +80,12 @@
         return remote(e_both.at[pl.ds(b * rows + batch, rows)], e_loc.at[b, k], e_send, e_sem.at[b % 2, k], sum_peer(k, -1))
 
     def pick_tokens():
-        n_words = emit_ref.shape[1]
-
-        def turn(first, count):
-            tile = emit_ref[:, pl.ds(first, count)].astype(F32) * LIFT
-            by_word[pl.ds(first, count), :] = tile.T
-
-        def turn_tiles(i, carry):
-            turn(pl.multiple_of(i * SB, SB), SB)
-            return carry
-
-        lax.fori_loop(0, n_words // SB, turn_tiles, 0, unroll=2)
-        if n_words % SB:
-            turn(n_words // SB * SB, n_words % SB)
+        def widen(i, carry):
+            some = pl.ds(pl.multiple_of(i * batch, batch), batch)
+            by_word[some, :] = emit_ref[some, :].astype(F32) * LIFT
+            return carry
+
+        lax.fori_loop(0, emit_ref.shape[0] // batch, widen, 0, unroll=5)
 
         def pick(t, carry):
             for b in range(batch):
@@ -391,10 +384,10 @@
                 dma((2, 2)), dma, dma((2,)), dma, dma((2,)), dma, dma((2,)), dma, dma((2,)), dma((2,)),
             ],
             compiler_params=pltpu.CompilerParams(collective_id=0, has_side_effects=True,
-                                                 vmem_limit_bytes=48 * 1024 * 1024),
+                                                 vmem_limit_bytes=36 * 1024 * 1024),
             cost_estimate=pl.CostEstimate(flops=2 * batch * (n_steps - 1) * n_sum * k_rows * cols,
                                           bytes_accessed=n_sum * k_rows * cols * 2, transcendentals=0),
-        )(a_blk, emit_blk, init_blk[None, :], tokens, lengths[None, :])
+        )(a_blk, emit_blk.T, init_blk[None, :], tokens, lengths[None, :])
         return ll[0], alpha
 
     return jax.shard_map(local_forward, mesh=mesh, in_specs=(P('rows', None, 'states'), P(vec_axes, None), P(vec_axes), P('seqs', None), P('seqs')), out_specs=(P('seqs'), P('seqs', vec_axes)), check_vma=False)

time: 974 us -> 969 us (level)
  no operation moved by 1% of the time
where the time goes in v11:
time: 969 us
  Pallas kernels  964 us (99%)
    pallas_call x1, Pallas kernels, local_forward(): pl.pallas_call(functools.partial(forward_kernel, CHIPS, n_steps, block),...  964 us

profile of v11, /device:TPU:1, one launch (start us, length us, event | category | flops | bytes accessed | tf_op | source)
XLA Modules:
  0.0 969.2 jit_solution(7832680864111749203)
XLA Ops:
  0.6 0.0 copy-start
  0.6 0.0 copy-start.1
  0.7 0.0 copy-start.2
  0.7 0.0 copy-start.3
  0.7 2.9 copy.9
  3.6 0.1 copy-done
  3.6 0.0 copy-done.1
  3.6 0.0 copy-done.2
  3.6 0.0 copy-done.3
  3.6 964.5 %shard_map.68 = (f32[16,128]{1,0:T(8,128)S(1)}, f32[1,16]{1,0:T(1,128)S(1)}) custom-call(bf16[8192,256]{1,0:T(8,128)(2,1)S(1)} %bitcast.8, bf16[10000,128]{1,0:T(8,128)(2,1)S(1)} %bitcast.9, f32[1,128]{1,0:T(1,128)S(1)} %bitcast.10, s32[16,128]{1,0:T(8,128)S(1)} %copy-done.1, s32[1,16]{1,0:T(1,128)S(1)} %bitcast.11), custom_call_target="tpu_custom_call" | custom-call | flops 17045651456 | bytes 8388608 | tf_op jit(solution)/shard_map/pallas_call | solution.py:356
  968.1 0.5 copy.12
  968.6 0.6 copy.13
Async XLA Ops:
  0.6 3.0 copy-start
  0.6 3.0 copy-start.1
  0.7 3.0 copy-start.2
  0.7 3.0 copy-start.3

commit v12 on v11

--- a/solution.py
+++ b/solution.py
@@ -105,7 +105,7 @@
     def helper():
         announce(me, 1)
         pl.semaphore_wait(barrier, n_sum)
-        for k in range(n_sum):
+        for k in range(n_sum // 2):
             start_a(0, k)
         e_both[pl.ds(n_steps * batch, batch), :] = jnp.zeros((batch, 2 * SB), BF16)
         pick_tokens()
@@ -118,6 +118,8 @@
         wait_bytes(e_both.at[every, pl.ds(SB, SB)], e_pair)
         for k in range(n_sum):
             e_copy(0, k).start()
+        for k in range(n_sum // 2, n_sum):
+            start_a(0, k)
         wait_bytes(e_loc.at[0], e_send)
 
         def send_part(i, carry):

time: 969 us -> 969 us (level)
  no operation moved by 1% of the time
where the time goes in v12:
time: 969 us
  Pallas kernels  964 us (99%)
    pallas_call x1, Pallas kernels, local_forward(): pl.pallas_call(functools.partial(forward_kernel, CHIPS, n_steps, block),...  964 us

profile of v12, /device:TPU:1, one launch (start us, length us, event | category | flops | bytes accessed | tf_op | source)
XLA Modules:
  0.0 969.2 jit_solution(6702218586338114838)
XLA Ops:
  0.6 0.0 copy-start
  0.6 0.0 copy-start.1
  0.7 0.0 copy-start.2
  0.7 0.0 copy-start.3
  0.7 2.9 copy.9
  3.6 0.1 copy-done
  3.6 0.0 copy-done.1
  3.6 0.0 copy-done.2
  3.6 0.0 copy-done.3
  3.6 964.4 %shard_map.68 = (f32[16,128]{1,0:T(8,128)S(1)}, f32[1,16]{1,0:T(1,128)S(1)}) custom-call(bf16[8192,256]{1,0:T(8,128)(2,1)S(1)} %bitcast.8, bf16[10000,128]{1,0:T(8,128)(2,1)S(1)} %bitcast.9, f32[1,128]{1,0:T(1,128)S(1)} %bitcast.10, s32[16,128]{1,0:T(8,128)S(1)} %copy-done.1, s32[1,16]{1,0:T(1,128)S(1)} %bitcast.11), custom_call_target="tpu_custom_call" | custom-call | flops 17045651456 | bytes 8388608 | tf_op jit(solution)/shard_map/pallas_call | solution.py:358
  968.1 0.5 copy.12
  968.6 0.6 copy.13
Async XLA Ops:
  0.6 3.0 copy-start
  0.6 3.0 copy-start.1
  0.7 3.0 copy-start.2
  0.7 3.0 copy-start.3

commit v13 on v12

--- a/solution.py
+++ b/solution.py
@@ -105,7 +105,7 @@
     def helper():
         announce(me, 1)
         pl.semaphore_wait(barrier, n_sum)
-        for k in range(n_sum // 2):
+        for k in range(1, n_sum, 2):
             start_a(0, k)
         e_both[pl.ds(n_steps * batch, batch), :] = jnp.zeros((batch, 2 * SB), BF16)
         pick_tokens()
@@ -118,7 +118,7 @@
         wait_bytes(e_both.at[every, pl.ds(SB, SB)], e_pair)
         for k in range(n_sum):
             e_copy(0, k).start()
-        for k in range(n_sum // 2, n_sum):
+        for k in range(0, n_sum, 2):
             start_a(0, k)
         wait_bytes(e_loc.at[0], e_send)
 
@@ -205,7 +205,7 @@
         for k in range(n_sum):
             announce(sum_peer(k), 0)
         pl.semaphore_wait(barrier, n_sum + n_gather - 1)
-        for k in range(1, n_sum):
+        for k in [*range(1, n_sum, 2), *range(2, n_sum, 2)]:
             start_a(1, k)
         for src, to in a_rows(me, 1):
             pltpu.make_async_copy(src, a_loc.at[0, to], own_sem.at[1]).start()
@@ -227,7 +227,8 @@
         wait_bytes(p_in.at[0, peers], p_send)
         wait_bytes(a_loc.at[0, pl.ds(0, half)], own_sem.at[1])
 
-        def first_w(k, carry):
+        def first_w(i, carry):
+            k = 2 * i + 1 - (n_sum + 1) * (i // (n_sum // 2))
             wait_bytes(a_loc.at[k, pl.ds(0, half)], a_sem.at[k, 0])
 
             @pl.when(k > 0)
@@ -324,15 +325,15 @@
         lax.fori_loop(0, n_steps - 1, one_step, 0)
         last = (n_steps - 1) % 2
         c_row, inv = norm(last)
-        wait_near(last)
-        wait_far(last)
         keep(n_steps - 1, last, c_row, inv)
-        wait_bytes(r_in.at[last, others], g_send)
-        wait_bytes(c_in.at[last, others], c_send)
         result = [remote(alpha_acc.at[0], fin_alpha, f_send.at[0], f_recv.at[0], me, to=0),
                   remote(ll_acc, fin_ll, f_send.at[1], f_recv.at[1], me, to=0)]
         for copy in result:
             copy.start()
+        wait_near(last)
+        wait_far(last)
+        wait_bytes(r_in.at[last, others], g_send)
+        wait_bytes(c_in.at[last, others], c_send)
         alpha_ref[...] = alpha_acc[1]
         ll_ref[...] = ll_acc[:, :batch]
         for copy in result:

time: 969 us -> 970 us (level)
  no operation moved by 1% of the time
where the time goes in v13:
time: 970 us
  Pallas kernels  965 us (99%)
    pallas_call x1, Pallas kernels, local_forward(): pl.pallas_call(functools.partial(forward_kernel, CHIPS, n_steps, block),...  965 us

profile of v13, /device:TPU:1, one launch (start us, length us, event | category | flops | bytes accessed | tf_op | source)
XLA Modules:
  0.0 969.6 jit_solution(11073469990993645050)
XLA Ops:
  0.6 0.0 copy-start
  0.6 0.0 copy-start.1
  0.7 0.0 copy-start.2
  0.7 0.0 copy-start.3
  0.7 2.9 copy.9
  3.6 0.1 copy-done
  3.6 0.0 copy-done.1
  3.6 0.0 copy-done.2
  3.6 0.0 copy-done.3
  3.6 964.8 %shard_map.68 = (f32[16,128]{1,0:T(8,128)S(1)}, f32[1,16]{1,0:T(1,128)S(1)}) custom-call(bf16[8192,256]{1,0:T(8,128)(2,1)S(1)} %bitcast.8, bf16[10000,128]{1,0:T(8,128)(2,1)S(1)} %bitcast.9, f32[1,128]{1,0:T(1,128)S(1)} %bitcast.10, s32[16,128]{1,0:T(8,128)S(1)} %copy-done.1, s32[1,16]{1,0:T(1,128)S(1)} %bitcast.11), custom_call_target="tpu_custom_call" | custom-call | flops 17045651456 | bytes 8388608 | tf_op jit(solution)/shard_map/pallas_call | solution.py:359
  968.5 0.5 copy.12
  969.0 0.6 copy.13
Async XLA Ops:
  0.6 3.0 copy-start
  0.6 3.0 copy-start.1
  0.7 3.0 copy-start.2
  0.7 3.0 copy-start.3

commit v14 on v13

--- a/solution.py
+++ b/solution.py
@@ -205,7 +205,7 @@
         for k in range(n_sum):
             announce(sum_peer(k), 0)
         pl.semaphore_wait(barrier, n_sum + n_gather - 1)
-        for k in [*range(1, n_sum, 2), *range(2, n_sum, 2)]:
+        for k in range(1, n_sum, 2):
             start_a(1, k)
         for src, to in a_rows(me, 1):
             pltpu.make_async_copy(src, a_loc.at[0, to], own_sem.at[1]).start()
@@ -223,6 +223,8 @@
         p_in[0, group] = as_row(r_in[0, 0, 0] + r_in[0, 0, 1])
         start_parts(0)
         start_gather(0)
+        for k in range(2, n_sum, 2):
+            start_a(1, k)
         finish_norm(0)
         wait_bytes(p_in.at[0, peers], p_send)
         wait_bytes(a_loc.at[0, pl.ds(0, half)], own_sem.at[1])

time: 970 us -> 974 us (level)
  no operation moved by 1% of the time
where the time goes in v14:
time: 974 us
  Pallas kernels  969 us (99%)
    pallas_call x1, Pallas kernels, local_forward(): pl.pallas_call(functools.partial(forward_kernel, CHIPS, n_steps, block),...  969 us

profile of v14, /device:TPU:1, one launch (start us, length us, event | category | flops | bytes accessed | tf_op | source)
XLA Modules:
  0.0 973.5 jit_solution(11329134988096433645)
XLA Ops:
  0.6 0.0 copy-start
  0.6 0.0 copy-start.1
  0.7 0.0 copy-start.2
  0.7 0.0 copy-start.3
  0.7 2.9 copy.9
  3.6 0.1 copy-done
  3.6 0.0 copy-done.1
  3.6 0.0 copy-done.2
  3.6 0.0 copy-done.3
  3.6 968.8 %shard_map.68 = (f32[16,128]{1,0:T(8,128)S(1)}, f32[1,16]{1,0:T(1,128)S(1)}) custom-call(bf16[8192,256]{1,0:T(8,128)(2,1)S(1)} %bitcast.8, bf16[10000,128]{1,0:T(8,128)(2,1)S(1)} %bitcast.9, f32[1,128]{1,0:T(1,128)S(1)} %bitcast.10, s32[16,128]{1,0:T(8,128)S(1)} %copy-done.1, s32[1,16]{1,0:T(1,128)S(1)} %bitcast.11), custom_call_target="tpu_custom_call" | custom-call | flops 17045651456 | bytes 8388608 | tf_op jit(solution)/shard_map/pallas_call | solution.py:361
  972.4 0.5 copy.12
  972.9 0.6 copy.13
Async XLA Ops:
  0.6 3.0 copy-start
  0.6 3.0 copy-start.1
  0.7 3.0 copy-start.2
  0.7 3.0 copy-start.3

commit v15 on v13

--- a/solution.py
+++ b/solution.py
@@ -205,7 +205,7 @@
         for k in range(n_sum):
             announce(sum_peer(k), 0)
         pl.semaphore_wait(barrier, n_sum + n_gather - 1)
-        for k in [*range(1, n_sum, 2), *range(2, n_sum, 2)]:
+        for k in [*range(1, n_sum, 2), *range(2, n_sum - 2, 2)]:
             start_a(1, k)
         for src, to in a_rows(me, 1):
             pltpu.make_async_copy(src, a_loc.at[0, to], own_sem.at[1]).start()
@@ -223,6 +223,7 @@
         p_in[0, group] = as_row(r_in[0, 0, 0] + r_in[0, 0, 1])
         start_parts(0)
         start_gather(0)
+        start_a(1, n_sum - 2)
         finish_norm(0)
         wait_bytes(p_in.at[0, peers], p_send)
         wait_bytes(a_loc.at[0, pl.ds(0, half)], own_sem.at[1])

time: 970 us -> 970 us (level)
  no operation moved by 1% of the time
where the time goes in v15:
time: 970 us
  Pallas kernels  965 us (99%)
    pallas_call x1, Pallas kernels, local_forward(): pl.pallas_call(functools.partial(forward_kernel, CHIPS, n_steps, block),...  965 us

profile of v15, /device:TPU:1, one launch (start us, length us, event | category | flops | bytes accessed | tf_op | source)
XLA Modules:
  0.0 969.6 jit_solution(7894991740033419442)
XLA Ops:
  0.6 0.0 copy-start
  0.6 0.0 copy-start.1
  0.7 0.0 copy-start.2
  0.7 0.0 copy-start.3
  0.7 2.9 copy.9
  3.6 0.1 copy-done
  3.6 0.0 copy-done.1
  3.6 0.0 copy-done.2
  3.6 0.0 copy-done.3
  3.6 964.9 %shard_map.68 = (f32[16,128]{1,0:T(8,128)S(1)}, f32[1,16]{1,0:T(1,128)S(1)}) custom-call(bf16[8192,256]{1,0:T(8,128)(2,1)S(1)} %bitcast.8, bf16[10000,128]{1,0:T(8,128)(2,1)S(1)} %bitcast.9, f32[1,128]{1,0:T(1,128)S(1)} %bitcast.10, s32[16,128]{1,0:T(8,128)S(1)} %copy-done.1, s32[1,16]{1,0:T(1,128)S(1)} %bitcast.11), custom_call_target="tpu_custom_call" | custom-call | flops 17045651456 | bytes 8388608 | tf_op jit(solution)/shard_map/pallas_call | solution.py:360
  968.5 0.5 copy.12
  969.0 0.6 copy.13
Async XLA Ops:
  0.6 3.0 copy-start
  0.6 3.0 copy-start.1
  0.7 3.0 copy-start.2
  0.7 3.0 copy-start.3

commit v16 on v12

--- a/solution.py
+++ b/solution.py
@@ -85,7 +85,7 @@
             by_word[some, :] = emit_ref[some, :].astype(F32) * LIFT
             return carry
 
-        lax.fori_loop(0, emit_ref.shape[0] // batch, widen, 0, unroll=5)
+        lax.fori_loop(0, emit_ref.shape[0] // batch, widen, 0, unroll=25)
 
         def pick(t, carry):
             for b in range(batch):
@@ -93,7 +93,7 @@
             e_half[pl.ds(pl.multiple_of(t * batch, batch), batch), :] = picked[t].astype(BF16)
             return carry
 
-        lax.fori_loop(0, n_steps, pick, 0)
+        lax.fori_loop(0, n_steps, pick, 0, unroll=4)
         r0_own[...] = picked[0] * init_ref[...]
 
     barrier = pltpu.get_barrier_semaphore()

time: 969 us -> 970 us (level)
  no operation moved by 1% of the time
where the time goes in v16:
time: 970 us; the launch traced here: 969 us
  Pallas kernels  965 us (99%)
    pallas_call x1, Pallas kernels, local_forward(): pl.pallas_call(functools.partial(forward_kernel, CHIPS, n_steps, block),...  965 us

profile of v16, /device:TPU:1, one launch (start us, length us, event | category | flops | bytes accessed | tf_op | source)
XLA Modules:
  0.0 969.4 jit_solution(6348526358463883991)
XLA Ops:
  0.6 0.0 copy-start
  0.6 0.0 copy-start.1
  0.7 0.0 copy-start.2
  0.7 0.0 copy-start.3
  0.7 2.9 copy.9
  3.6 0.1 copy-done
  3.6 0.0 copy-done.1
  3.6 0.0 copy-done.2
  3.6 0.0 copy-done.3
  3.6 964.7 %shard_map.68 = (f32[16,128]{1,0:T(8,128)S(1)}, f32[1,16]{1,0:T(1,128)S(1)}) custom-call(bf16[8192,256]{1,0:T(8,128)(2,1)S(1)} %bitcast.8, bf16[10000,128]{1,0:T(8,128)(2,1)S(1)} %bitcast.9, f32[1,128]{1,0:T(1,128)S(1)} %bitcast.10, s32[16,128]{1,0:T(8,128)S(1)} %copy-done.1, s32[1,16]{1,0:T(1,128)S(1)} %bitcast.11), custom_call_target="tpu_custom_call" | custom-call | flops 17045651456 | bytes 8388608 | tf_op jit(solution)/shard_map/pallas_call | solution.py:358
  968.3 0.5 copy.12
  968.8 0.6 copy.13
Async XLA Ops:
  0.6 3.0 copy-start
  0.6 3.0 copy-start.1
  0.7 3.0 copy-start.2
  0.7 3.0 copy-start.3
